TPU v7x, 32 devices: a whole 2x2x4 slice. The times are simulated.
32 devices in a mesh: edp: 8 (over z, core), ep: 4 (over y, x).
Axes of the slice: x: 2, y: 2, z: 4, core: 2. Of those that a mesh axis runs over, the one named last changes fastest.
Arguments:
- route_ids: int32 [4096, 8], P(('edp', 'ep')), may hold values from 0 to 127, all different within a row; in each aligned block of 128 rows (0 to 127, 128 to 255, ...) at most 16 rows name the same one
- route_weights: float32 [4096, 8], P(('edp', 'ep')), may hold values from 0.02 to 0.5
- hidden: bfloat16 [8, 4, 4, 16, 384], P('edp', 'ep'), may hold values from -6 to 6
- down_weight: bfloat16 [4, 384, 2048], P('ep', 'edp'), may hold values from -0.3125 to 0.3125
- cotangent: bfloat16 [4096, 2048], P(('edp', 'ep')), may hold values from -6 to 6
Outputs:
- layer_out: bfloat16 [4096, 2048], P(('edp', 'ep'))
- route_grad: float32 [4096, 8], P(('edp', 'ep'))
- hidden_grad: bfloat16 [8, 4, 4, 16, 384], P('edp', 'ep')
- weight_grad: float32 [4, 384, 2048], P('ep', 'edp')
Inputs may be any that keep to these rules, and one draw needn't show every extreme that they name: `route_ids`: each row names 8 different experts; in the 128 rows of one device no expert is named by more than 16 rows.
All inputs are finite; a program needn't handle non-finite values.
Results may differ from a plain program's by a relative error of at most 0.0049.
Values may be sent and summed in bfloat16 or wider, within the bound.
No kernel may reach another device: no remote copies, remote signals or barrier semaphores. Data moves between devices by JAX's collectives and lax.ppermute only.
A program may use at most 64 MiB of HBM per device.

v0:
```python
import jax
import jax.numpy as jnp
from jax import lax
from jax.sharding import PartitionSpec as P


def local(route_ids, route_weights, hidden, down_weight, cotangent):
    experts_here = lax.axis_size("ep")
    capacity = hidden.shape[3]
    features = cotangent.shape[1]
    hidden_width = hidden.shape[4]
    slot_total = hidden.shape[2] * capacity
    hidden_rows = hidden.reshape(slot_total, hidden_width)
    shard_rows = down_weight[0]
    weight_full = lax.all_gather(shard_rows, "edp", axis=0, tiled=True)
    expert_out = jnp.dot(hidden_rows, weight_full, preferred_element_type=jnp.float32)
    sent_out = expert_out.astype(jnp.bfloat16).reshape(hidden.shape[2], capacity, features)
    arrived = lax.all_to_all(sent_out, "ep", split_axis=0, concat_axis=0, tiled=True)
    arrived_rows = arrived.reshape(experts_here * capacity, features)
    labels = jnp.arange(experts_here, dtype=jnp.int32)
    onehot = jnp.sum((route_ids[:, :, None] == labels).astype(jnp.int32), axis=1)
    preceding = jnp.cumsum(onehot, axis=0) - onehot
    flight = route_ids < experts_here
    expert = jnp.where(flight, route_ids, 0)
    slot_rank = jnp.take_along_axis(preceding, expert, axis=1)
    slot_index = expert * capacity + slot_rank
    mixing = jnp.where(flight, route_weights, jnp.float32(0.0))
    positions = jnp.arange(experts_here * capacity, dtype=jnp.int32)
    matches = (slot_index[None, :, :] == positions[:, None, None]) & flight[None, :, :]
    combine_table = jnp.sum(jnp.where(matches, mixing[None, :, :], jnp.float32(0.0)), axis=2)
    arrived_f32 = arrived_rows.astype(jnp.float32)
    combined = lax.dot_general(
        combine_table,
        arrived_f32,
        (((0,), (0,)), ((), ())),
        precision=lax.Precision.HIGHEST,
        preferred_element_type=jnp.float32,
    )
    scores = lax.dot_general(
        cotangent, arrived_rows, (((1,), (1,)), ((), ())), preferred_element_type=jnp.float32
    )
    route_grad = jnp.where(
        flight, jnp.take_along_axis(scores, slot_index, axis=1), jnp.float32(0.0)
    )
    selector = jnp.any(matches, axis=2).astype(jnp.bfloat16)
    slot_weight = jnp.sum(combine_table, axis=1)
    gathered_cot = jnp.dot(selector, cotangent, preferred_element_type=jnp.float32)
    slot_grad = (
        (gathered_cot * slot_weight[:, None])
        .astype(jnp.bfloat16)
        .reshape(experts_here, capacity, features)
    )
    returned = lax.all_to_all(slot_grad, "ep", split_axis=0, concat_axis=0, tiled=True)
    grad_rows = returned.reshape(slot_total, features)
    hidden_grad = lax.dot_general(
        grad_rows, weight_full, (((1,), (1,)), ((), ())), preferred_element_type=jnp.float32
    )
    hidden_grad = hidden_grad.astype(jnp.bfloat16).reshape(hidden.shape)
    weight_grad = lax.psum_scatter(
        lax.dot_general(
            hidden_rows, grad_rows, (((0,), (0,)), ((), ())), preferred_element_type=jnp.float32
        ),
        "edp",
        scatter_dimension=0,
        tiled=True,
    )
    return (combined.astype(jnp.bfloat16), route_grad, hidden_grad, weight_grad[None])


def solution(mesh):
    in_specs = (
        P(("edp", "ep"), None),
        P(("edp", "ep"), None),
        P("edp", "ep", None, None, None),
        P("ep", "edp", None),
        P(("edp", "ep"), None),
    )
    out_specs = (
        P(("edp", "ep"), None),
        P(("edp", "ep"), None),
        P("edp", "ep", None, None, None),
        P("ep", "edp", None),
    )
    return jax.shard_map(local, mesh=mesh, in_specs=in_specs, out_specs=out_specs, check_vma=False)
```

profile of v0, /device:TPU:0, one launch (start us, length us, event | category | flops | bytes accessed | tf_op | source)
XLA Modules:
  0.0 119.3 jit_solution(11195226603537378797)
XLA Ops:
  7.2 0.0 copy-start
  7.2 0.0 all-gather.3.cloned.1.call-start
  7.2 0.7 all-gather.3.cloned.1.call-update
  7.9 0.8 copy.26
  8.7 0.7 convert_reduce_fusion
  9.4 0.1 copy.28
  9.5 0.2 reduce_window_sum.11
  9.8 0.1 reshape.57
  9.8 0.0 copy-start.2
  9.9 7.1 %gather_fusion = s32[1024]{0:T(1024)S(1)} fusion(s32[128,4]{1,0:T(8,128)S(1)} %sub.3, s32[1024]{0:T(1024)S(1)} %reshape.57), kind=kCustom, calls=%fused_computation | custom fusion | bytes 16384 | tf_op jit(solution)/shard_map/jit(take_along_axis)/gather | solution.py:25
  16.9 0.0 copy-start.3
  16.9 0.1 reshape.60
  17.0 20.6 %all-gather.3.cloned.1.call-done = bf16[1,384,2048]{2,1,0:T(8,128)(2,1)} async-done(((bf16[1,48,2048]{2,1,0:T(8,128)(2,1)}), bf16[1,384,2048]{2,1,0:T(8,128)(2,1)}) %all-gather.3.cloned.1.call-update) | async-done | bytes 1572880 | tf_op jit(solution)/shard_map/all_gather | solution.py:15
  37.7 0.0 copy-done.2
  37.7 2.5 %convolution_convert_fusion.1 = bf16[64,2048]{1,0:T(8,128)(2,1)} fusion(bf16[64,384]{1,0:T(8,128)(2,1)S(1)} %bitcast.43, bf16[1,384,2048]{2,1,0:T(8,128)(2,1)} %all-gather.3.cloned.1.call-done), kind=kOutput, calls=%fused_computation.6 | convolution fusion | flops 100794368 | bytes 1884160 | tf_op jit(solution)/shard_map/dot_general | solution.py:16
  40.2 3.7 %all-to-all-start = ((bf16[4,16,2048]{2,1,0:T(8,128)(2,1)}), bf16[4,16,2048]{2,1,0:T(8,128)(2,1)S(1)}, u32[]{:S(2)}, u32[]{:S(2)}) async-start(bf16[4,16,2048]{2,1,0:T(8,128)(2,1)} %bitcast.3), calls=%async_computation | async-start | bytes 524288 | tf_op jit(solution)/shard_map/all_to_all | solution.py:18
  43.8 0.0 reduce-scatter.4.cloned.1.call-start
  43.8 0.1 bitcast_or_fusion
  43.9 0.1 copy.31
  43.9 0.0 copy-done.3
  43.9 0.1 copy.32
  44.1 0.1 reshape.63
  44.2 0.1 fusion.8
  44.3 5.2 %all-to-all-done = bf16[4,16,2048]{2,1,0:T(8,128)(2,1)S(1)} async-done(((bf16[4,16,2048]{2,1,0:T(8,128)(2,1)}), bf16[4,16,2048]{2,1,0:T(8,128)(2,1)S(1)}, u32[]{:S(2)}, u32[]{:S(2)}) %all-to-all-start) | async-done | bytes 262176 | tf_op jit(solution)/shard_map/all_to_all | solution.py:18
  49.6 0.0 copy-done
  49.6 0.3 convolution_bitcast_fusion.1
  49.9 7.0 %gather_fusion.1 = f32[1024]{0:T(1024)S(1)} fusion(f32[128,64]{0,1:T(8,128)S(1)} %convolution_bitcast_fusion.1, s32[1024]{0:T(1024)S(1)} %reshape.63), kind=kCustom, calls=%fused_computation.1 | custom fusion | bytes 16384 | tf_op jit(solution)/shard_map/jit(take_along_axis)/gather | solution.py:43
  56.9 0.1 reshape.66
  57.1 0.6 select_reduce_fusion
  57.7 0.2 fusion
  57.9 8.1 %all_to_all.10 = bf16[4,16,2048]{2,1,0:T(8,128)(2,1)S(1)} all-to-all(bf16[4,16,2048]{2,1,0:T(8,128)(2,1)S(1)} %bitcast.42), channel_id=1, replica_groups=mesh['edp'=8,'ep'=4] {'ep'}, dimensions={0} | all-to-all | bytes 524288 | tf_op jit(solution)/shard_map/all_to_all | solution.py:53
  66.0 2.3 %convolution_bitcast_fusion = f32[384,2048]{0,1:T(8,128)} fusion(bf16[64,2048]{1,0:T(8,128)(2,1)S(1)} %bitcast.40, bf16[64,384]{1,0:T(8,128)(2,1)S(1)} %bitcast.44), kind=kOutput, calls=%fused_computation.2 | convolution fusion | flops 100663296 | bytes 3457024 | tf_op jit(solution)/shard_map/dot_general | solution.py:60
  68.3 3.5 %copy.36 = f32[384,2048]{1,0:T(8,128)} copy(f32[384,2048]{0,1:T(8,128)} %convolution_bitcast_fusion) | data formatting | bytes 6291456
  71.8 0.0 copy-start.1
  71.8 0.0 reduce-scatter.4.cloned.1.call-update
  71.9 0.7 copy.34
  72.5 1.4 %convolution_convert_fusion = bf16[128,2048]{1,0:T(8,128)(2,1)} fusion(f32[64,128]{1,0:T(8,128)S(1)} %get-tuple-element.21, bf16[64,2048]{1,0:T(8,128)(2,1)S(1)} %bitcast.39), kind=kOutput, calls=%fused_computation.3 | convolution fusion | flops 201588736 | bytes 819200 | tf_op jit(solution)/shard_map/dot_general | solution.py:32
  73.9 0.0 copy-done.1
  73.9 1.2 %fusion.4 = bf16[64,384]{1,0:T(8,128)(2,1)} fusion(bf16[64,2048]{1,0:T(8,128)(2,1)S(1)} %bitcast.41, bf16[1,384,2048]{2,1,0:T(8,128)(2,1)S(1)} %copy-done.1), kind=kOutput, calls=%fused_computation.10 | convolution fusion | flops 100687872 | bytes 1884160 | tf_op jit(solution)/shard_map/dot_general | solution.py:55
  75.2 34.9 %reduce-scatter.4.cloned.1.call-done = f32[48,2048]{1,0:T(8,128)} async-done(((f32[384,2048]{1,0:T(8,128)}), f32[48,2048]{1,0:T(8,128)}) %reduce-scatter.4.cloned.1.call-update) | async-done | bytes 393232
  110.1 1.3 %copy.37 = f32[48,2048]{0,1:T(8,128)S(1)} copy(f32[48,2048]{1,0:T(8,128)} %reduce-scatter.4.cloned.1.call-done) | data formatting | bytes 786432
  111.4 1.1 copy.35
  (5 shorter events, 0.2 us)
Async XLA Ops:
  7.2 42.4 %copy-start = (bf16[128,2048]{1,0:T(8,128)(2,1)S(1)}, bf16[128,2048]{1,0:T(8,128)(2,1)}, u32[]{:S(2)}) copy-start(bf16[128,2048]{1,0:T(8,128)(2,1)} %param.9) | copy-start | bytes 1572868
  7.2 30.5 %all-gather.3.cloned.1.call-start = ((), (), s32[]{:S(2)}) async-start(), calls=%async_computation.3 | async-start | bytes 1769472 | tf_op jit(solution)/shard_map/all_gather | solution.py:15
  9.8 27.8 %copy-start.2 = (bf16[1,1,4,16,384]{4,3,2,1,0:T(8,128)(2,1)S(1)}, bf16[1,1,4,16,384]{4,3,2,1,0:T(8,128)(2,1)}, u32[]{:S(2)}) copy-start(bf16[1,1,4,16,384]{4,3,2,1,0:T(8,128)(2,1)} %param.7) | copy-start | bytes 147460
  16.9 27.0 %copy-start.3 = (f32[128,8]{0,1:T(8,128)S(1)}, f32[128,8]{0,1:T(8,128)}, u32[]{:S(2)}) copy-start(f32[128,8]{0,1:T(8,128)} %param.6) | copy-start | bytes 12292
  40.2 9.4 %all-to-all-start = ((bf16[4,16,2048]{2,1,0:T(8,128)(2,1)}), bf16[4,16,2048]{2,1,0:T(8,128)(2,1)S(1)}, u32[]{:S(2)}, u32[]{:S(2)}) async-start(bf16[4,16,2048]{2,1,0:T(8,128)(2,1)} %bitcast.3), calls=%async_computation | async-start | bytes 524288 | tf_op jit(solution)/shard_map/all_to_all | solution.py:18
  43.8 66.3 %reduce-scatter.4.cloned.1.call-start = ((), (), s32[]{:S(2)}) async-start(), calls=%async_computation.4 | async-start | bytes 3538944
  71.8 2.1 %copy-start.1 = (bf16[1,384,2048]{2,1,0:T(8,128)(2,1)S(1)}, bf16[1,384,2048]{2,1,0:T(8,128)(2,1)}, u32[]{:S(2)}) copy-start(bf16[1,384,2048]{2,1,0:T(8,128)(2,1)} %all-gather.3.cloned.1.call-done) | copy-start | bytes 4718596
Sparse Core Ops, SparseCore 0:
  9.6 27.9 all-gather.2
  72.0 38.0 reduce-scatter.3
where the time goes:
time: 120 us; the launch traced here: 119 us
  waiting for transfers between devices  61.5 us (51%)
  local copies, waits for them, and re-layouts  22.2 us (18%)
  between operations  14.1 us (12%)
  blocking collectives  8.11 us (7%)
  matrix products  7.98 us (7%)
  starting transfers between devices  3.69 us (3%)
  other arithmetic  1.7 us (1%)
    unnamed x3, waiting for transfers between devices  35.6 us
    all_gather x1, waiting for transfers between devices, local(): weight_full = lax.all_gather(shard_rows, 'edp', axis=0, tiled=True)  20.6 us
    all_to_all x1, blocking collectives, local(): lax.all_to_all(slot_grad, 'ep', split_axis=0, concat_axis=0, tiled=True)  8.11 us
    unnamed x14, local copies, waits for them, and re-layouts  7.5 us
    gather x3, local copies, waits for them, and re-layouts, local(): slot_rank = jnp.take_along_axis(preceding, expert, axis=1)  7.24 us
    gather x3, local copies, waits for them, and re-layouts, local(): jnp.take_along_axis(scores, slot_index, axis=1)  7.19 us
    all_to_all x1, waiting for transfers between devices, local(): lax.all_to_all(sent_out, 'ep', split_axis=0, concat_axis=0, tiled=True)  5.25 us
    all_to_all x1, starting transfers between devices, local(): lax.all_to_all(sent_out, 'ep', split_axis=0, concat_axis=0, tiled=True)  3.65 us
  transfers between devices with their start and end apart: 3, of which 3 were waited for; matrix products, arithmetic and copies ran while one was open for 11% of the time, Pallas kernels for 0%

commit v1 on v0

v1 whole, which is shorter than its diff:
```python
import functools

import jax
import jax.numpy as jnp
from jax import lax
from jax.experimental import pallas as pl
from jax.experimental.pallas import tpu as pltpu
from jax.sharding import Mesh
from jax.sharding import PartitionSpec as P

BF16 = jnp.bfloat16
F32 = jnp.float32
NN = (((1,), (0,)), ((), ()))
NT = (((1,), (1,)), ((), ()))
TN = (((0,), (0,)), ((), ()))


def dot(a, b, dims):
    return lax.dot_general(a, b, dims, preferred_element_type=F32)


def call(body, outs, scratch=(), flops=0, name=None):
    size = sum(o.size * o.dtype.itemsize for o in jax.tree.leaves(outs))
    return pl.pallas_call(
        body,
        out_shape=outs,
        scratch_shapes=scratch,
        name=name,
        cost_estimate=pl.CostEstimate(flops=flops, bytes_accessed=2 * size, transcendentals=0),
    )


def sds(shape, dtype):
    return jax.ShapeDtypeStruct(shape, dtype)


def aligned(index, size, unit):
    return pl.ds(pl.multiple_of(index * size, unit), size)


def halves_body(w_ref, same_ref, cross_ref):
    h = lax.axis_index("h")
    half = same_ref.shape[1]
    same_ref[...] = w_ref[:, aligned(h, half, 128)]
    cross_ref[...] = w_ref[:, aligned(1 - h, half, 128)]


def route_body(experts, capacity, ids_ref, weight_ref, cot_ref, sent_ref, table_ref, index_ref):
    ids = ids_ref[...]
    weights = weight_ref[...]
    tokens = ids.shape[1]
    half = sent_ref.shape[2]
    row = lax.broadcasted_iota(jnp.int32, (tokens, tokens), 0)
    col = lax.broadcasted_iota(jnp.int32, (tokens, tokens), 1)
    earlier = jnp.where(row < col, 1.0, 0.0).astype(BF16)
    named = [jnp.sum(jnp.where(ids == e, 1.0, 0.0), axis=0, keepdims=True) for e in range(experts)]
    mixing = [jnp.sum(jnp.where(ids == e, weights, 0.0), axis=0, keepdims=True) for e in range(experts)]
    preceding = dot(jnp.concatenate(named, axis=0).astype(BF16), earlier, NN)
    slot = lax.broadcasted_iota(jnp.int32, (capacity, tokens), 0).astype(F32)
    chosen, combine = [], []
    index = jnp.full(ids.shape, -1.0, F32)
    for e in range(experts):
        rank = preceding[e : e + 1]
        match = jnp.where(rank == slot, 1.0, 0.0) * named[e]
        chosen.append(match)
        combine.append(match * mixing[e])
        index = jnp.where(ids == e, rank + float(e * capacity), index)
    index_ref[...] = index
    chosen = jnp.concatenate(chosen, axis=0)
    combine = jnp.concatenate(combine, axis=0)
    slots = chosen.shape[0]
    slot_weight = jnp.sum(combine, axis=1, keepdims=True)
    high = combine.astype(BF16)
    rest = combine - high.astype(F32)
    middle = rest.astype(BF16)
    table_ref[0:slots] = high
    table_ref[slots : 2 * slots] = middle
    table_ref[2 * slots : 3 * slots] = (rest - middle.astype(F32)).astype(BF16)
    gathered = dot(chosen.astype(BF16), cot_ref[...], NN)
    value = (gathered * slot_weight).astype(BF16)
    for g in range(2):
        for e in range(experts):
            sent_ref[g * experts + e] = value[e * capacity : (e + 1) * capacity, g * half : (g + 1) * half]


def expert_body(moves, groups, *refs):
    count = len(moves)
    blocks = refs[: 2 * count]
    own_ref, pair_ref, out_ref, full_ref, hid_ref, stage_ref = refs[2 * count :]
    q, h, c = lax.axis_index("q"), lax.axis_index("h"), lax.axis_index("c")
    rows = blocks[0].shape[0]
    slots = own_ref.shape[0]
    for i, (dq, dh) in enumerate(moves):
        source = (lax.rem(q + (groups - dq), groups) * 2 + lax.rem(h + dh, 2)) * 2
        stage_ref[aligned(source + c, rows, 8), :] = blocks[i][...].astype(stage_ref.dtype)
        stage_ref[aligned(source + 1 - c, rows, 8), :] = blocks[count + i][...].astype(stage_ref.dtype)
    hid_ref[aligned(h, slots, 16), :] = own_ref[...]
    hid_ref[aligned(1 - h, slots, 16), :] = pair_ref[...]
    full = stage_ref[...].astype(BF16)
    full_ref[...] = full
    out_ref[...] = dot(hid_ref[...], full, NN).astype(BF16).reshape(out_ref.shape)


def hidden_grad_body(grad_ref, full_ref, keep_ref, send_ref):
    h = lax.axis_index("h")
    n = grad_ref.shape[0] // 2
    flat = (n * grad_ref.shape[1], grad_ref.shape[2])
    full = full_ref[...]
    keep_ref[...] = dot(grad_ref[pl.ds(h * n, n)].reshape(flat), full, NT)
    send_ref[...] = dot(grad_ref[pl.ds((1 - h) * n, n)].reshape(flat), full, NT).astype(BF16)


def weight_grad_body(moves, groups, own_ref, h_ref, c_ref, hc_ref, grad_ref, partner_ref, *refs):
    count = len(moves)
    outs, (hid_ref, total_ref) = refs[:count], refs[count:]
    q, h, c = lax.axis_index("q"), lax.axis_index("h"), lax.axis_index("c")
    slots = own_ref.shape[0]
    rows = outs[0].shape[0]
    hid_ref[aligned(h, slots, 16), :] = own_ref[...]
    hid_ref[aligned(1 - h, slots, 16), :] = h_ref[...]
    hid_ref[aligned(2 + h, slots, 16), :] = c_ref[...]
    hid_ref[aligned(3 - h, slots, 16), :] = hc_ref[...]
    flat = (2 * slots, grad_ref.shape[2])
    grads = jnp.concatenate([grad_ref[...].reshape(flat), partner_ref[...].reshape(flat)], axis=0)
    total_ref[...] = dot(hid_ref[...], grads, TN)
    for (dq, dh), out in zip(moves, outs, strict=True):
        target = (lax.rem(q + dq, groups) * 2 + lax.rem(h + dh, 2)) * 2 + c
        out[...] = total_ref[aligned(target, rows, 8), :].astype(out.dtype)


def combine_body(arrived_ref, table_ref, index_ref, cot_ref, layer_ref, route_ref):
    n, capacity, half = arrived_ref.shape
    slots = n // 2 * capacity
    scores = None
    for g in range(2):
        rows = arrived_ref[g * (n // 2) : (g + 1) * (n // 2)].reshape(slots, half)
        mixed = dot(table_ref[...], jnp.concatenate([rows] * 3, axis=0), TN)
        layer_ref[:, g * half : (g + 1) * half] = mixed.astype(BF16)
        part = dot(rows, cot_ref[:, g * half : (g + 1) * half], NT)
        scores = part if scores is None else scores + part
    position = lax.broadcasted_iota(jnp.int32, scores.shape, 0).astype(F32)
    for k in range(index_ref.shape[0]):
        hit = position == index_ref[k : k + 1]
        route_ref[k : k + 1] = jnp.sum(jnp.where(hit, scores, 0.0), axis=0, keepdims=True)


def finish_body(moves, keep_ref, arrived_ref, *refs):
    count = len(moves)
    terms, (hidden_ref, weight_ref) = refs[:count], refs[count:]
    h = lax.axis_index("h")
    half = terms[0].shape[1]
    hidden_ref[...] = (keep_ref[...] + arrived_ref[...].astype(F32)).astype(BF16)
    for side in range(2):
        total = None
        for (_, dh), term in zip(moves, terms, strict=True):
            if dh == side:
                value = term[...].astype(F32)
                total = value if total is None else total + value
        weight_ref[:, aligned(h if side == 0 else 1 - h, half, 128)] = total


def local(route_ids, route_weights, hidden, down_weight, cotangent):
    groups = lax.axis_size("q")
    experts = lax.axis_size("ep")
    tokens, features = cotangent.shape
    capacity, width = hidden.shape[3], hidden.shape[4]
    rows = down_weight.shape[1]
    slots = experts * capacity
    half = features // 2
    moves = [(0, 0), (0, 1)] + [(dq, dh) for dq in range(1, groups) for dh in range(2)]
    chips = ("q", "h")
    swap = [(0, 1), (1, 0)]

    def move(x, step):
        dq, dh = step
        pairs = [(a * 2 + b, (a + dq) % groups * 2 + (b + dh) % 2) for a in range(groups) for b in range(2)]
        return lax.ppermute(x, chips, pairs)

    def swap_core(x):
        return lax.ppermute(x, "c", swap)

    shard = down_weight[0]
    piece = sds((rows, half), BF16)
    same, cross = call(halves_body, (piece, piece), name="halves")(shard)
    blocks = [same] + [move(cross if dh else same, (dq, dh)) for dq, dh in moves[1:]]
    blocks = blocks + [swap_core(b) for b in blocks]

    own = hidden.reshape(slots, width)
    pair = lax.ppermute(own, "h", swap)
    partner = swap_core(own)
    diagonal = lax.ppermute(own, ("h", "c"), [(i, 3 - i) for i in range(4)])

    parts = sds((2 * experts, capacity, half), BF16)
    sent, table, index = call(
        functools.partial(route_body, experts, capacity),
        (parts, sds((3 * slots, tokens), BF16), sds((route_ids.shape[1], tokens), F32)),
        flops=2 * slots * tokens * features,
        name="route",
    )(route_ids.T, route_weights.T, cotangent)
    grads = lax.all_to_all(sent, ("h", "ep"), split_axis=0, concat_axis=0, tiled=True)
    partner_grads = swap_core(grads)

    weight_out = call(
        functools.partial(weight_grad_body, moves, groups),
        tuple(sds((rows, half), BF16 if i else F32) for i in range(len(moves))),
        [pltpu.VMEM((4 * slots, width), BF16), pltpu.VMEM((width, half), F32)],
        flops=2 * 4 * slots * width * half,
        name="weight_grad",
    )(own, pair, partner, diagonal, grads, partner_grads)
    terms = [weight_out[0]] + [move(x, step) for x, step in zip(weight_out[1:], moves[1:], strict=True)]

    expert_out, full = call(
        functools.partial(expert_body, moves, groups),
        (parts, sds((width, half), BF16)),
        [pltpu.VMEM((2 * slots, width), BF16), pltpu.VMEM((width, half), BF16 if rows % 16 == 0 else F32)],
        flops=2 * 2 * slots * width * half,
        name="expert",
    )(*blocks, own, pair)
    arrived = lax.all_to_all(expert_out, ("h", "ep"), split_axis=0, concat_axis=0, tiled=True)

    keep, give = call(
        hidden_grad_body,
        (sds((slots, width), F32), sds((slots, width), BF16)),
        flops=2 * 2 * slots * width * half,
        name="hidden_grad",
    )(grads, full)
    taken = lax.ppermute(give, "h", swap)

    layer_out, route_grad = call(
        combine_body,
        (sds((tokens, features), BF16), sds((route_ids.shape[1], tokens), F32)),
        flops=2 * 4 * slots * tokens * features,
        name="combine",
    )(arrived, table, index, cotangent)

    hidden_grad, weight_grad = call(
        functools.partial(finish_body, moves),
        (sds((slots, width), BF16), sds((rows, features), F32)),
        flops=rows * features,
        name="finish",
    )(keep, taken, *terms)
    return layer_out, route_grad.T, hidden_grad.reshape(hidden.shape), weight_grad[None]


def solution(mesh):
    edp, ep = mesh.shape["edp"], mesh.shape["ep"]
    fine = Mesh(mesh.devices.reshape(edp // 4, 2, 2, ep), ("q", "h", "c", "ep"))
    group = ("q", "h", "c")
    tokens = P(group + ("ep",), None)
    slots = P(group, "ep", None, None, None)
    weights = P("ep", group, None)
    return jax.shard_map(
        local,
        mesh=fine,
        in_specs=(tokens, tokens, slots, weights, tokens),
        out_specs=(tokens, tokens, slots, weights),
        check_vma=False,
    )
```

time: 120 us -> 58.9 us (0.49)
  waiting for transfers between devices: 61.5 us -> 15.3 us
  starting transfers between devices: 3.69 us -> 22.9 us
  local copies, waits for them, and re-layouts: 22.2 us -> 4.04 us
  Pallas kernels: 0 us -> 15.3 us
  between operations: 14.1 us -> 0.79 us
  blocking collectives: 8.11 us -> 0 us
  matrix products: 7.98 us -> 0 us
  other arithmetic: 1.7 us -> 0 us
    unnamed x3 -> x0, waiting for transfers between devices: 35.6 us -> none
    all_gather x1 -> x0, waiting for transfers between devices: 20.6 us -> none  [local(): weight_full = lax.all_gather(shard_rows, 'edp', axis=0, tiled=True)]
    ppermute x0 -> x15, waiting for transfers between devices: none -> 15.3 us  [the longest x6 7.27 us: move(): return lax.ppermute(x, chips, pairs)]
    pallas_call x0 -> x7, Pallas kernels: none -> 15.3 us  [the longest x1 2.44 us: local(): call(hidden_grad_body, (sds((slots, width), F32), sds((slots, width), BF1...]
    gather x6 -> x0, local copies, waits for them, and re-layouts: 14.4 us -> none  [the longest x3 7.24 us: local(): slot_rank = jnp.take_along_axis(preceding, expert, axis=1)]
    ppermute x0 -> x15, starting transfers between devices: none -> 12.6 us  [the longest x6 8.99 us: move(): return lax.ppermute(x, chips, pairs)]
    all_to_all x1 -> x0, blocking collectives: 8.11 us -> none  [local(): lax.all_to_all(slot_grad, 'ep', split_axis=0, concat_axis=0, tiled=True)]
    dot_general x6 -> x0, matrix products: 7.98 us -> none  [the longest x1 2.51 us: local(): jnp.dot(hidden_rows, weight_full, preferred_element_type=jnp.float32)]
  transfers between devices with their start and end apart: 3 -> 17, of which waited for: 3 -> 6; matrix products, arithmetic and copies ran while one was open for 11% -> 0% of each run, Pallas kernels for 0% -> 19%
where the time goes in v1:
time: 58.9 us; the launch traced here: 58.3 us
  starting transfers between devices  22.9 us (39%)
  Pallas kernels  15.3 us (26%)
  waiting for transfers between devices  15.3 us (26%)
  local copies, waits for them, and re-layouts  4.04 us (7%)
  between operations  0.79 us (1%)
    ppermute x6, starting transfers between devices, move(): return lax.ppermute(x, chips, pairs)  8.99 us
    ppermute x6, waiting for transfers between devices, move(): return lax.ppermute(x, chips, pairs)  7.27 us
    all_to_all x1, starting transfers between devices, local(): lax.all_to_all(sent, ('h', 'ep'), split_axis=0, concat_axis=0, tiled=True)  6.21 us
    all_to_all x1, starting transfers between devices, local(): lax.all_to_all(expert_out, ('h', 'ep'), split_axis=0, concat_axis=0, tile...  4.1 us
    unnamed x38, local copies, waits for them, and re-layouts  4.04 us
    ppermute x1, waiting for transfers between devices, local(): pair = lax.ppermute(own, 'h', swap)  3.49 us
    ppermute x1, waiting for transfers between devices, local(): taken = lax.ppermute(give, 'h', swap)  2.66 us
    pallas_call x1, Pallas kernels, local(): call(hidden_grad_body, (sds((slots, width), F32), sds((slots, width), BF1...  2.44 us
  transfers between devices with their start and end apart: 17, of which 6 were waited for; matrix products, arithmetic and copies ran while one was open for 0% of the time, Pallas kernels for 19%

profile of v1, /device:TPU:0, one launch (start us, length us, event | category | flops | bytes accessed | tf_op | source)
XLA Modules:
  0.0 58.3 jit_solution(7641213798748723167)
XLA Ops:
  0.6 2.1 %route.1 = (bf16[8,16,1024]{2,1,0:T(8,128)(2,1)}, bf16[192,128]{1,0:T(8,128)(2,1)}, f32[8,128]{1,0:T(8,128)}) custom-call(s32[8,128]{1,0:T(8,128)} %bitcast.13, f32[8,128]{1,0:T(8,128)} %bitcast.14, bf16[128,2048]{1,0:T(8,128)(2,1)} %cot_ref.3), custom_call_target="tpu_custom_call" | custom-call | flops 33554432 | bytes 630784 | tf_op jit(solution)/shard_map/route/pallas_call | solution.py:194
  2.8 6.2 %all-to-all-start.1 = ((bf16[8,16,1024]{2,1,0:T(8,128)(2,1)}), bf16[8,16,1024]{2,1,0:T(8,128)(2,1)S(1)}, u32[]{:S(2)}, u32[]{:S(2)}) async-start(bf16[8,16,1024]{2,1,0:T(8,128)(2,1)} %get-tuple-element.28), calls=%async_computation.1 | async-start | bytes 524288 | tf_op jit(solution)/shard_map/all_to_all | solution.py:200
  9.0 1.6 %halves.1 = (bf16[48,1024]{1,0:T(8,128)(2,1)}, bf16[48,1024]{1,0:T(8,128)(2,1)}) custom-call(bf16[48,2048]{1,0:T(8,128)(2,1)} %bitcast.7), custom_call_target="tpu_custom_call" | custom-call | bytes 393216 | tf_op jit(solution)/shard_map/halves/pallas_call | solution.py:184
  10.6 2.6 %collective-permute-start.1 = (bf16[48,1024]{1,0:T(8,128)(2,1)}, bf16[48,1024]{1,0:T(8,128)(2,1)S(1)}, u32[]{:S(2)}, u32[]{:S(2)}) collective-permute-start(bf16[48,1024]{1,0:T(8,128)(2,1)} %get-tuple-element.21.refs_0_), channel_id=1, source_target_pairs={{0,16},{8,24},{16,0},{24,8},{1,17},{9,25},{17,1},{25,9},{2,18},{10... | collective-permute-start | bytes 294920 | tf_op jit(solution)/shard_map/ppermute | solution.py:177
  13.2 2.0 %collective-permute-start = (bf16[48,1024]{1,0:T(8,128)(2,1)}, bf16[48,1024]{1,0:T(8,128)(2,1)S(1)}, u32[]{:S(2)}, u32[]{:S(2)}) collective-permute-start(bf16[48,1024]{1,0:T(8,128)(2,1)} %get-tuple-element.22), channel_id=1, source_target_pairs={{0,8},{8,0},{16,24},{24,16},{1,9},{9,1},{17,25},{25,17},{2,10},{10... | collective-permute-start | bytes 294920 | tf_op jit(solution)/shard_map/ppermute | solution.py:177
  15.2 0.0 collective-permute-start.2
  15.2 0.0 collective-permute-start.3
  15.2 2.9 %collective-permute-done.1.refs_2_ = bf16[48,1024]{1,0:T(8,128)(2,1)S(1)} collective-permute-done((bf16[48,1024]{1,0:T(8,128)(2,1)}, bf16[48,1024]{1,0:T(8,128)(2,1)S(1)}, u32[]{:S(2)}, u32[]{:S(2)}) %collective-permute-start.1) | collective-permute-done | bytes 98336 | tf_op jit(solution)/shard_map/ppermute | solution.py:177
  18.1 0.0 collective-permute-start.5
  18.1 0.6 %collective-permute-done.refs_1_ = bf16[48,1024]{1,0:T(8,128)(2,1)S(1)} collective-permute-done((bf16[48,1024]{1,0:T(8,128)(2,1)}, bf16[48,1024]{1,0:T(8,128)(2,1)S(1)}, u32[]{:S(2)}, u32[]{:S(2)}) %collective-permute-start) | collective-permute-done | bytes 98336 | tf_op jit(solution)/shard_map/ppermute | solution.py:177
  18.8 0.0 collective-permute-start.4
  18.8 3.7 %collective-permute-done.2.refs_3_ = bf16[48,1024]{1,0:T(8,128)(2,1)S(1)} collective-permute-done((bf16[48,1024]{1,0:T(8,128)(2,1)}, bf16[48,1024]{1,0:T(8,128)(2,1)S(1)}, u32[]{:S(2)}, u32[]{:S(2)}) %collective-permute-start.2) | collective-permute-done | bytes 98336 | tf_op jit(solution)/shard_map/ppermute | solution.py:177
  22.5 0.0 collective-permute-start.6
  22.5 0.0 copy-done.12
  22.5 0.7 %collective-permute-start.7 = (bf16[64,384]{1,0:T(8,128)(2,1)S(1)}, bf16[64,384]{1,0:T(8,128)(2,1)S(1)}, u32[]{:S(2)}, u32[]{:S(2)}) collective-permute-start(bf16[64,384]{1,0:T(8,128)(2,1)S(1)} %bitcast.10), channel_id=1, source_target_pairs={{0,8},{8,0},{1,9},{9,1},{2,10},{10,2},{3,11},{11,3},{4,12},{12,4},... | collective-permute-start | bytes 147464 | tf_op jit(solution)/shard_map/ppermute | solution.py:189
  23.2 3.5 %collective-permute-done.7.refs_9_.h_ref = bf16[64,384]{1,0:T(8,128)(2,1)S(1)} collective-permute-done((bf16[64,384]{1,0:T(8,128)(2,1)S(1)}, bf16[64,384]{1,0:T(8,128)(2,1)S(1)}, u32[]{:S(2)}, u32[]{:S(2)}) %collective-permute-start.7) | collective-permute-done | bytes 49184 | tf_op jit(solution)/shard_map/ppermute | solution.py:189
  26.7 0.0 collective-permute-done.3.refs_4_
  26.7 0.0 collective-permute-done.5.refs_6_
  26.7 0.0 copy-start.9
  26.7 0.0 collective-permute-done.4.refs_5_
  26.7 0.0 copy-start.10
  26.7 0.0 collective-permute-done.6.refs_7_
  26.7 0.0 copy-done.2
  26.7 0.0 copy-done.3
  26.7 0.0 copy-done.5
  26.7 0.5 copy-done.14
  27.3 0.0 copy-done.7
  27.3 0.0 copy-done.9
  27.3 0.0 copy-done.10
  27.4 0.6 %copy-done.11 = bf16[48,1024]{1,0:T(8,128)(2,1)} copy-done((bf16[48,1024]{1,0:T(8,128)(2,1)}, bf16[48,1024]{1,0:T(8,128)(2,1)S(1)}, u32[]{:S(2)}) %copy-start.11) | copy-done | bytes 98328
  28.0 2.3 %expert.1 = (bf16[8,16,1024]{2,1,0:T(8,128)(2,1)}, bf16[384,1024]{1,0:T(8,128)(2,1)}) custom-call(bf16[48,1024]{1,0:T(8,128)(2,1)} %get-tuple-element.21.refs_0_, bf16[48,1024]{1,0:T(8,128)(2,1)} %copy-done.3, bf16[48,1024]{1,0:T(8,128)(2,1)} %copy-done.2, bf16[48,1024]{1,0:T(8,128)(2,1)} %copy-done.5, bf16[48,1024]{1,0:T(8,128)(2,1)} %copy-done.7, ...), custom_call_target="tpu_custom_call" | custom-call | flops 100663296 | bytes 2097152 | tf_op jit(solution)/shard_map/expert/pallas_call | solution.py:212
  30.4 0.0 all-to-all-done.1.grad_ref
  30.4 0.0 copy-start.13
  30.4 4.1 %all-to-all-start = ((bf16[8,16,1024]{2,1,0:T(8,128)(2,1)}), bf16[8,16,1024]{2,1,0:T(8,128)(2,1)S(1)}, u32[]{:S(2)}, u32[]{:S(2)}) async-start(bf16[8,16,1024]{2,1,0:T(8,128)(2,1)} %get-tuple-element.23), calls=%async_computation | async-start | bytes 524288 | tf_op jit(solution)/shard_map/all_to_all | solution.py:219
  34.5 0.0 copy-done.1
  34.5 0.1 collective-permute-start.11
  34.6 0.0 copy-done.13
  34.6 2.0 %collective-permute-start.10 = (bf16[64,384]{1,0:T(8,128)(2,1)S(1)}, bf16[64,384]{1,0:T(8,128)(2,1)S(1)}, u32[]{:S(2)}, u32[]{:S(2)}) collective-permute-start(bf16[64,384]{1,0:T(8,128)(2,1)S(1)} %bitcast.11), channel_id=1, source_target_pairs={{0,12},{4,8},{8,4},{12,0},{1,13},{5,9},{9,5},{13,1},{2,14},{6,10},... | collective-permute-start | bytes 147464 | tf_op jit(solution)/shard_map/ppermute | solution.py:191
  36.6 0.1 collective-permute-start.9
  36.7 1.8 %collective-permute-done.10.hc_ref = bf16[64,384]{1,0:T(8,128)(2,1)S(1)} collective-permute-done((bf16[64,384]{1,0:T(8,128)(2,1)S(1)}, bf16[64,384]{1,0:T(8,128)(2,1)S(1)}, u32[]{:S(2)}, u32[]{:S(2)}) %collective-permute-start.10) | collective-permute-done | bytes 49184 | tf_op jit(solution)/shard_map/ppermute | solution.py:191
  38.6 0.0 collective-permute-done.9.c_ref
  38.6 0.0 collective-permute-done.11.partner_ref
  38.6 0.6 %copy-done.17 = bf16[64,384]{1,0:T(8,128)(2,1)} copy-done((bf16[64,384]{1,0:T(8,128)(2,1)}, bf16[64,384]{1,0:T(8,128)(2,1)S(1)}, u32[]{:S(2)}) %copy-start.17) | copy-done | bytes 49176
  39.2 0.0 copy-done.18
  39.2 0.7 %copy-done.16 = bf16[8,16,1024]{2,1,0:T(8,128)(2,1)} copy-done((bf16[8,16,1024]{2,1,0:T(8,128)(2,1)}, bf16[8,16,1024]{2,1,0:T(8,128)(2,1)S(1)}, u32[]{:S(2)}) %copy-start.16) | copy-done | bytes 262168
  39.9 2.4 %weight_grad.1 = (f32[48,1024]{1,0:T(8,128)}, bf16[48,1024]{1,0:T(8,128)(2,1)}, bf16[48,1024]{1,0:T(8,128)(2,1)}, bf16[48,1024]{1,0:T(8,128)(2,1)}) custom-call(bf16[64,384]{1,0:T(8,128)(2,1)} %bitcast.9, bf16[64,384]{1,0:T(8,128)(2,1)} %copy-done.14, bf16[64,384]{1,0:T(8,128)(2,1)} %copy-done.18, bf16[64,384]{1,0:T(8,128)(2,1)} %copy-done.17, ...), custom_call_target="tpu_custom_call" | custom-call | flops 201326592 | bytes 983040 | tf_op jit(solution)/shard_map/weight_grad/pallas_call | solution.py:203
  42.3 1.6 %collective-permute-start.12 = (bf16[48,1024]{1,0:T(8,128)(2,1)}, bf16[48,1024]{1,0:T(8,128)(2,1)S(1)}, u32[]{:S(2)}, u32[]{:S(2)}) collective-permute-start(bf16[48,1024]{1,0:T(8,128)(2,1)} %get-tuple-element.33), channel_id=1, source_target_pairs={{0,8},{8,0},{16,24},{24,16},{1,9},{9,1},{17,25},{25,17},{2,10},{10... | collective-permute-start | bytes 294920 | tf_op jit(solution)/shard_map/ppermute | solution.py:177
  43.9 2.3 %collective-permute-start.13 = (bf16[48,1024]{1,0:T(8,128)(2,1)}, bf16[48,1024]{1,0:T(8,128)(2,1)S(1)}, u32[]{:S(2)}, u32[]{:S(2)}) collective-permute-start(bf16[48,1024]{1,0:T(8,128)(2,1)} %get-tuple-element.34), channel_id=1, source_target_pairs={{0,16},{8,24},{16,0},{24,8},{1,17},{9,25},{17,1},{25,9},{2,18},{10... | collective-permute-start | bytes 294920 | tf_op jit(solution)/shard_map/ppermute | solution.py:177
  46.3 0.4 collective-permute-start.14
  46.7 2.4 %hidden_grad.1 = (f32[64,384]{1,0:T(8,128)}, bf16[64,384]{1,0:T(8,128)(2,1)}) custom-call(bf16[8,16,1024]{2,1,0:T(8,128)(2,1)} %copy-done.1, bf16[384,1024]{1,0:T(8,128)(2,1)} %get-tuple-element.29.full_ref), custom_call_target="tpu_custom_call" | custom-call | flops 100663296 | bytes 294912 | tf_op jit(solution)/shard_map/hidden_grad/pallas_call | solution.py:221
  49.1 0.7 %collective-permute-start.8 = (bf16[64,384]{1,0:T(8,128)(2,1)}, bf16[64,384]{1,0:T(8,128)(2,1)S(1)}, u32[]{:S(2)}, u32[]{:S(2)}) collective-permute-start(bf16[64,384]{1,0:T(8,128)(2,1)} %get-tuple-element.31), channel_id=1, source_target_pairs={{0,8},{8,0},{1,9},{9,1},{2,10},{10,2},{3,11},{11,3},{4,12},{12,4},... | collective-permute-start | bytes 147464 | tf_op jit(solution)/shard_map/ppermute | solution.py:227
  49.8 0.0 all-to-all-done.arrived_ref
  49.8 0.7 %copy-done = bf16[8,16,1024]{2,1,0:T(8,128)(2,1)} copy-done((bf16[8,16,1024]{2,1,0:T(8,128)(2,1)}, bf16[8,16,1024]{2,1,0:T(8,128)(2,1)S(1)}, u32[]{:S(2)}) %copy-start) | copy-done | bytes 262168
  50.5 2.4 %combine.1 = (bf16[128,2048]{1,0:T(8,128)(2,1)}, f32[8,128]{1,0:T(8,128)}) custom-call(bf16[8,16,1024]{2,1,0:T(8,128)(2,1)} %copy-done, bf16[192,128]{1,0:T(8,128)(2,1)} %get-tuple-element.24.table_ref, f32[8,128]{1,0:T(8,128)} %get-tuple-element.25.index_ref, bf16[128,2048]{1,0:T(8,128)(2,1)} %cot_ref.3), custom_call_target="tpu_custom_call" | custom-call | flops 134217728 | bytes 1056768 | tf_op jit(solution)/shard_map/combine/pallas_call | solution.py:229
  52.9 2.7 %collective-permute-done.8.arrived_ref = bf16[64,384]{1,0:T(8,128)(2,1)S(1)} collective-permute-done((bf16[64,384]{1,0:T(8,128)(2,1)}, bf16[64,384]{1,0:T(8,128)(2,1)S(1)}, u32[]{:S(2)}, u32[]{:S(2)}) %collective-permute-start.8) | collective-permute-done | bytes 49184 | tf_op jit(solution)/shard_map/ppermute | solution.py:227
  55.6 0.0 collective-permute-done.12.refs_1_
  55.6 0.0 collective-permute-done.13.refs_2_
  55.6 0.0 copy-start.6
  55.6 0.0 collective-permute-done.14.refs_3_
  55.6 0.6 copy-done.15
  56.2 0.0 copy-done.4
  56.3 0.0 copy-done.6
  56.3 0.0 copy-done.8
  56.3 2.0 %finish.1 = (bf16[64,384]{1,0:T(8,128)(2,1)}, f32[48,2048]{1,0:T(8,128)}) custom-call(f32[64,384]{1,0:T(8,128)} %get-tuple-element.30.keep_ref, bf16[64,384]{1,0:T(8,128)(2,1)} %copy-done.15, f32[48,1024]{1,0:T(8,128)} %get-tuple-element.32.refs_0_, bf16[48,1024]{1,0:T(8,128)(2,1)} %copy-done.4, bf16[48,1024]{1,0:T(8,128)(2,1)} %copy-done.6, ...), custom_call_target="tpu_custom_call" | custom-call | flops 98304 | bytes 884736 | tf_op jit(solution)/shard_map/finish/pallas_call | solution.py:236
  (15 shorter events, 0.0 us)
Async XLA Ops:
  2.8 27.6 %all-to-all-start.1 = ((bf16[8,16,1024]{2,1,0:T(8,128)(2,1)}), bf16[8,16,1024]{2,1,0:T(8,128)(2,1)S(1)}, u32[]{:S(2)}, u32[]{:S(2)}) async-start(bf16[8,16,1024]{2,1,0:T(8,128)(2,1)} %get-tuple-element.28), calls=%async_computation.1 | async-start | bytes 524288 | tf_op jit(solution)/shard_map/all_to_all | solution.py:200
  9.0 13.5 %copy-start.12 = (bf16[1,1,4,16,384]{4,3,2,1,0:T(8,128)(2,1)S(1)}, bf16[1,1,4,16,384]{4,3,2,1,0:T(8,128)(2,1)}, u32[]{:S(2)}) copy-start(bf16[1,1,4,16,384]{4,3,2,1,0:T(8,128)(2,1)} %param.7) | copy-start | bytes 147460
  10.6 7.5 %collective-permute-start.1 = (bf16[48,1024]{1,0:T(8,128)(2,1)}, bf16[48,1024]{1,0:T(8,128)(2,1)S(1)}, u32[]{:S(2)}, u32[]{:S(2)}) collective-permute-start(bf16[48,1024]{1,0:T(8,128)(2,1)} %get-tuple-element.21.refs_0_), channel_id=1, source_target_pairs={{0,16},{8,24},{16,0},{24,8},{1,17},{9,25},{17,1},{25,9},{2,18},{10... | collective-permute-start | bytes 294920 | tf_op jit(solution)/shard_map/ppermute | solution.py:177
  13.2 5.6 %collective-permute-start = (bf16[48,1024]{1,0:T(8,128)(2,1)}, bf16[48,1024]{1,0:T(8,128)(2,1)S(1)}, u32[]{:S(2)}, u32[]{:S(2)}) collective-permute-start(bf16[48,1024]{1,0:T(8,128)(2,1)} %get-tuple-element.22), channel_id=1, source_target_pairs={{0,8},{8,0},{16,24},{24,16},{1,9},{9,1},{17,25},{25,17},{2,10},{10... | collective-permute-start | bytes 294920 | tf_op jit(solution)/shard_map/ppermute | solution.py:177
  15.2 7.3 %collective-permute-start.2 = (bf16[48,1024]{1,0:T(8,128)(2,1)}, bf16[48,1024]{1,0:T(8,128)(2,1)S(1)}, u32[]{:S(2)}, u32[]{:S(2)}) collective-permute-start(bf16[48,1024]{1,0:T(8,128)(2,1)} %get-tuple-element.22), channel_id=1, source_target_pairs={{0,24},{8,16},{16,8},{24,0},{1,25},{9,17},{17,9},{25,1},{2,26},{10... | collective-permute-start | bytes 294920 | tf_op jit(solution)/shard_map/ppermute | solution.py:177
  15.2 11.5 %collective-permute-start.3 = (bf16[48,1024]{1,0:T(8,128)(2,1)}, bf16[48,1024]{1,0:T(8,128)(2,1)S(1)}, u32[]{:S(2)}, u32[]{:S(2)}) collective-permute-start(bf16[48,1024]{1,0:T(8,128)(2,1)} %get-tuple-element.21.refs_0_), channel_id=1, source_target_pairs={{0,4},{4,0},{1,5},{5,1},{2,6},{6,2},{3,7},{7,3},{8,12},{12,8},{9,1... | collective-permute-start | bytes 294920 | tf_op jit(solution)/shard_map/ppermute | solution.py:180
  18.1 8.6 %copy-start.2 = (bf16[48,1024]{1,0:T(8,128)(2,1)}, bf16[48,1024]{1,0:T(8,128)(2,1)S(1)}, u32[]{:S(2)}) copy-start(bf16[48,1024]{1,0:T(8,128)(2,1)S(1)} %collective-permute-done.1.refs_2_) | copy-start | bytes 294916
  18.1 8.5 %collective-permute-start.5 = (bf16[48,1024]{1,0:T(8,128)(2,1)S(1)}, bf16[48,1024]{1,0:T(8,128)(2,1)S(1)}, u32[]{:S(2)}, u32[]{:S(2)}) collective-permute-start(bf16[48,1024]{1,0:T(8,128)(2,1)S(1)} %collective-permute-done.1.refs_2_), channel_id=1, source_target_pairs={{0,4},{4,0},{1,5},{5,1},{2,6},{6,2},{3,7},{7,3},{8,12},{12,8},{9,1... | collective-permute-start | bytes 294920 | tf_op jit(solution)/shard_map/ppermute | solution.py:180
  18.8 8.0 %copy-start.3 = (bf16[48,1024]{1,0:T(8,128)(2,1)}, bf16[48,1024]{1,0:T(8,128)(2,1)S(1)}, u32[]{:S(2)}) copy-start(bf16[48,1024]{1,0:T(8,128)(2,1)S(1)} %collective-permute-done.refs_1_) | copy-start | bytes 294916
  18.8 7.9 %collective-permute-start.4 = (bf16[48,1024]{1,0:T(8,128)(2,1)S(1)}, bf16[48,1024]{1,0:T(8,128)(2,1)S(1)}, u32[]{:S(2)}, u32[]{:S(2)}) collective-permute-start(bf16[48,1024]{1,0:T(8,128)(2,1)S(1)} %collective-permute-done.refs_1_), channel_id=1, source_target_pairs={{0,4},{4,0},{1,5},{5,1},{2,6},{6,2},{3,7},{7,3},{8,12},{12,8},{9,1... | collective-permute-start | bytes 294920 | tf_op jit(solution)/shard_map/ppermute | solution.py:180
  22.5 4.2 %copy-start.5 = (bf16[48,1024]{1,0:T(8,128)(2,1)}, bf16[48,1024]{1,0:T(8,128)(2,1)S(1)}, u32[]{:S(2)}) copy-start(bf16[48,1024]{1,0:T(8,128)(2,1)S(1)} %collective-permute-done.2.refs_3_) | copy-start | bytes 294916
  22.5 4.2 %collective-permute-start.6 = (bf16[48,1024]{1,0:T(8,128)(2,1)S(1)}, bf16[48,1024]{1,0:T(8,128)(2,1)S(1)}, u32[]{:S(2)}, u32[]{:S(2)}) collective-permute-start(bf16[48,1024]{1,0:T(8,128)(2,1)S(1)} %collective-permute-done.2.refs_3_), channel_id=1, source_target_pairs={{0,4},{4,0},{1,5},{5,1},{2,6},{6,2},{3,7},{7,3},{8,12},{12,8},{9,1... | collective-permute-start | bytes 294920 | tf_op jit(solution)/shard_map/ppermute | solution.py:180
  22.5 4.2 %collective-permute-start.7 = (bf16[64,384]{1,0:T(8,128)(2,1)S(1)}, bf16[64,384]{1,0:T(8,128)(2,1)S(1)}, u32[]{:S(2)}, u32[]{:S(2)}) collective-permute-start(bf16[64,384]{1,0:T(8,128)(2,1)S(1)} %bitcast.10), channel_id=1, source_target_pairs={{0,8},{8,0},{1,9},{9,1},{2,10},{10,2},{3,11},{11,3},{4,12},{12,4},... | collective-permute-start | bytes 147464 | tf_op jit(solution)/shard_map/ppermute | solution.py:189
  26.7 0.6 %copy-start.14 = (bf16[64,384]{1,0:T(8,128)(2,1)}, bf16[64,384]{1,0:T(8,128)(2,1)S(1)}, u32[]{:S(2)}) copy-start(bf16[64,384]{1,0:T(8,128)(2,1)S(1)} %collective-permute-done.7.refs_9_.h_ref) | copy-start | bytes 147460
  26.7 0.7 %copy-start.7 = (bf16[48,1024]{1,0:T(8,128)(2,1)}, bf16[48,1024]{1,0:T(8,128)(2,1)S(1)}, u32[]{:S(2)}) copy-start(bf16[48,1024]{1,0:T(8,128)(2,1)S(1)} %collective-permute-done.3.refs_4_) | copy-start | bytes 294916
  26.7 0.7 %copy-start.9 = (bf16[48,1024]{1,0:T(8,128)(2,1)}, bf16[48,1024]{1,0:T(8,128)(2,1)S(1)}, u32[]{:S(2)}) copy-start(bf16[48,1024]{1,0:T(8,128)(2,1)S(1)} %collective-permute-done.5.refs_6_) | copy-start | bytes 294916
  26.7 0.7 %copy-start.10 = (bf16[48,1024]{1,0:T(8,128)(2,1)}, bf16[48,1024]{1,0:T(8,128)(2,1)S(1)}, u32[]{:S(2)}) copy-start(bf16[48,1024]{1,0:T(8,128)(2,1)S(1)} %collective-permute-done.4.refs_5_) | copy-start | bytes 294916
  27.4 0.6 %copy-start.11 = (bf16[48,1024]{1,0:T(8,128)(2,1)}, bf16[48,1024]{1,0:T(8,128)(2,1)S(1)}, u32[]{:S(2)}) copy-start(bf16[48,1024]{1,0:T(8,128)(2,1)S(1)} %collective-permute-done.6.refs_7_) | copy-start | bytes 294916
  30.4 4.1 %copy-start.1 = (bf16[8,16,1024]{2,1,0:T(8,128)(2,1)}, bf16[8,16,1024]{2,1,0:T(8,128)(2,1)S(1)}, u32[]{:S(2)}) copy-start(bf16[8,16,1024]{2,1,0:T(8,128)(2,1)S(1)} %all-to-all-done.1.grad_ref) | copy-start | bytes 786436
  30.4 4.2 %copy-start.13 = (bf16[1,1,4,16,384]{4,3,2,1,0:T(8,128)(2,1)S(1)}, bf16[1,1,4,16,384]{4,3,2,1,0:T(8,128)(2,1)}, u32[]{:S(2)}) copy-start(bf16[1,1,4,16,384]{4,3,2,1,0:T(8,128)(2,1)} %param.7) | copy-start | bytes 147460
  30.4 19.5 %all-to-all-start = ((bf16[8,16,1024]{2,1,0:T(8,128)(2,1)}), bf16[8,16,1024]{2,1,0:T(8,128)(2,1)S(1)}, u32[]{:S(2)}, u32[]{:S(2)}) async-start(bf16[8,16,1024]{2,1,0:T(8,128)(2,1)} %get-tuple-element.23), calls=%async_computation | async-start | bytes 524288 | tf_op jit(solution)/shard_map/all_to_all | solution.py:219
  34.5 4.1 %collective-permute-start.11 = (bf16[8,16,1024]{2,1,0:T(8,128)(2,1)S(1)}, bf16[8,16,1024]{2,1,0:T(8,128)(2,1)S(1)}, u32[]{:S(2)}, u32[]{:S(2)}) collective-permute-start(bf16[8,16,1024]{2,1,0:T(8,128)(2,1)S(1)} %all-to-all-done.1.grad_ref), channel_id=1, source_target_pairs={{0,4},{4,0},{1,5},{5,1},{2,6},{6,2},{3,7},{7,3},{8,12},{12,8},{9,1... | collective-permute-start | bytes 786440 | tf_op jit(solution)/shard_map/ppermute | solution.py:180
  34.6 4.0 %collective-permute-start.10 = (bf16[64,384]{1,0:T(8,128)(2,1)S(1)}, bf16[64,384]{1,0:T(8,128)(2,1)S(1)}, u32[]{:S(2)}, u32[]{:S(2)}) collective-permute-start(bf16[64,384]{1,0:T(8,128)(2,1)S(1)} %bitcast.11), channel_id=1, source_target_pairs={{0,12},{4,8},{8,4},{12,0},{1,13},{5,9},{9,5},{13,1},{2,14},{6,10},... | collective-permute-start | bytes 147464 | tf_op jit(solution)/shard_map/ppermute | solution.py:191
  36.6 1.9 %collective-permute-start.9 = (bf16[64,384]{1,0:T(8,128)(2,1)S(1)}, bf16[64,384]{1,0:T(8,128)(2,1)S(1)}, u32[]{:S(2)}, u32[]{:S(2)}) collective-permute-start(bf16[64,384]{1,0:T(8,128)(2,1)S(1)} %bitcast.12), channel_id=1, source_target_pairs={{0,4},{4,0},{1,5},{5,1},{2,6},{6,2},{3,7},{7,3},{8,12},{12,8},{9,1... | collective-permute-start | bytes 147464 | tf_op jit(solution)/shard_map/ppermute | solution.py:180
  38.5 0.6 %copy-start.17 = (bf16[64,384]{1,0:T(8,128)(2,1)}, bf16[64,384]{1,0:T(8,128)(2,1)S(1)}, u32[]{:S(2)}) copy-start(bf16[64,384]{1,0:T(8,128)(2,1)S(1)} %collective-permute-done.10.hc_ref) | copy-start | bytes 147460
  38.6 0.7 %copy-start.18 = (bf16[64,384]{1,0:T(8,128)(2,1)}, bf16[64,384]{1,0:T(8,128)(2,1)S(1)}, u32[]{:S(2)}) copy-start(bf16[64,384]{1,0:T(8,128)(2,1)S(1)} %collective-permute-done.9.c_ref) | copy-start | bytes 147460
  39.2 0.7 %copy-start.16 = (bf16[8,16,1024]{2,1,0:T(8,128)(2,1)}, bf16[8,16,1024]{2,1,0:T(8,128)(2,1)S(1)}, u32[]{:S(2)}) copy-start(bf16[8,16,1024]{2,1,0:T(8,128)(2,1)S(1)} %collective-permute-done.11.partner_ref) | copy-start | bytes 786436
  42.3 13.3 %collective-permute-start.12 = (bf16[48,1024]{1,0:T(8,128)(2,1)}, bf16[48,1024]{1,0:T(8,128)(2,1)S(1)}, u32[]{:S(2)}, u32[]{:S(2)}) collective-permute-start(bf16[48,1024]{1,0:T(8,128)(2,1)} %get-tuple-element.33), channel_id=1, source_target_pairs={{0,8},{8,0},{16,24},{24,16},{1,9},{9,1},{17,25},{25,17},{2,10},{10... | collective-permute-start | bytes 294920 | tf_op jit(solution)/shard_map/ppermute | solution.py:177
  43.9 11.7 %collective-permute-start.13 = (bf16[48,1024]{1,0:T(8,128)(2,1)}, bf16[48,1024]{1,0:T(8,128)(2,1)S(1)}, u32[]{:S(2)}, u32[]{:S(2)}) collective-permute-start(bf16[48,1024]{1,0:T(8,128)(2,1)} %get-tuple-element.34), channel_id=1, source_target_pairs={{0,16},{8,24},{16,0},{24,8},{1,17},{9,25},{17,1},{25,9},{2,18},{10... | collective-permute-start | bytes 294920 | tf_op jit(solution)/shard_map/ppermute | solution.py:177
  46.3 9.4 %collective-permute-start.14 = (bf16[48,1024]{1,0:T(8,128)(2,1)}, bf16[48,1024]{1,0:T(8,128)(2,1)S(1)}, u32[]{:S(2)}, u32[]{:S(2)}) collective-permute-start(bf16[48,1024]{1,0:T(8,128)(2,1)} %get-tuple-element.35), channel_id=1, source_target_pairs={{0,24},{8,16},{16,8},{24,0},{1,25},{9,17},{17,9},{25,1},{2,26},{10... | collective-permute-start | bytes 294920 | tf_op jit(solution)/shard_map/ppermute | solution.py:177
  49.1 6.5 %collective-permute-start.8 = (bf16[64,384]{1,0:T(8,128)(2,1)}, bf16[64,384]{1,0:T(8,128)(2,1)S(1)}, u32[]{:S(2)}, u32[]{:S(2)}) collective-permute-start(bf16[64,384]{1,0:T(8,128)(2,1)} %get-tuple-element.31), channel_id=1, source_target_pairs={{0,8},{8,0},{1,9},{9,1},{2,10},{10,2},{3,11},{11,3},{4,12},{12,4},... | collective-permute-start | bytes 147464 | tf_op jit(solution)/shard_map/ppermute | solution.py:227
  49.8 0.7 %copy-start = (bf16[8,16,1024]{2,1,0:T(8,128)(2,1)}, bf16[8,16,1024]{2,1,0:T(8,128)(2,1)S(1)}, u32[]{:S(2)}) copy-start(bf16[8,16,1024]{2,1,0:T(8,128)(2,1)S(1)} %all-to-all-done.arrived_ref) | copy-start | bytes 786436
  55.6 0.6 %copy-start.15 = (bf16[64,384]{1,0:T(8,128)(2,1)}, bf16[64,384]{1,0:T(8,128)(2,1)S(1)}, u32[]{:S(2)}) copy-start(bf16[64,384]{1,0:T(8,128)(2,1)S(1)} %collective-permute-done.8.arrived_ref) | copy-start | bytes 147460
  55.6 0.6 %copy-start.4 = (bf16[48,1024]{1,0:T(8,128)(2,1)}, bf16[48,1024]{1,0:T(8,128)(2,1)S(1)}, u32[]{:S(2)}) copy-start(bf16[48,1024]{1,0:T(8,128)(2,1)S(1)} %collective-permute-done.12.refs_1_) | copy-start | bytes 294916
  55.6 0.7 %copy-start.6 = (bf16[48,1024]{1,0:T(8,128)(2,1)}, bf16[48,1024]{1,0:T(8,128)(2,1)S(1)}, u32[]{:S(2)}) copy-start(bf16[48,1024]{1,0:T(8,128)(2,1)S(1)} %collective-permute-done.13.refs_2_) | copy-start | bytes 294916
  55.6 0.7 %copy-start.8 = (bf16[48,1024]{1,0:T(8,128)(2,1)}, bf16[48,1024]{1,0:T(8,128)(2,1)S(1)}, u32[]{:S(2)}) copy-start(bf16[48,1024]{1,0:T(8,128)(2,1)S(1)} %collective-permute-done.14.refs_3_) | copy-start | bytes 294916

commit v2 on v1

v2 whole, which is shorter than its diff:
```python
import functools

import jax
import jax.numpy as jnp
from jax import lax
from jax.experimental import pallas as pl
from jax.experimental.pallas import tpu as pltpu
from jax.sharding import Mesh
from jax.sharding import PartitionSpec as P


LOAD_LIMIT = 16 * 2**20
BF16 = jnp.bfloat16
F32 = jnp.float32
NN = (((1,), (0,)), ((), ()))
NT = (((1,), (1,)), ((), ()))
TN = (((0,), (0,)), ((), ()))


def dot(a, b, dims):
    return lax.dot_general(a, b, dims, preferred_element_type=F32)


def call(body, outs, scratch=(), flops=0, fetched=False, limit=16 * 2**20):
    size = sum(o.size * o.dtype.itemsize for o in jax.tree.leaves(outs))
    space = pl.BlockSpec(memory_space=pltpu.VMEM)
    inputs = pl.BlockSpec(memory_space=pltpu.HBM) if fetched else space

    def run(*args):
        if fetched:
            args = [pltpu.with_memory_space_constraint(x, pltpu.HBM) for x in args]
        return pl.pallas_call(
            body,
            out_shape=outs,
            in_specs=[inputs] * len(args),
            out_specs=jax.tree.map(lambda _: space, outs),
            scratch_shapes=scratch,
            compiler_params=pltpu.CompilerParams(vmem_limit_bytes=limit),
            cost_estimate=pl.CostEstimate(flops=flops, bytes_accessed=2 * size, transcendentals=0),
        )(*args)

    return run


def sds(shape, dtype):
    return jax.ShapeDtypeStruct(shape, dtype)


def aligned(index, size, unit):
    return pl.ds(pl.multiple_of(index * size, unit), size)


def pack(block):
    rows = block.shape[0] // 2
    return jnp.concatenate([block[:rows], block[rows:]], axis=1)


def unpack(block, width):
    return jnp.concatenate([block[:, :width], block[:, width : 2 * width]], axis=0)


def load_body(w_hbm, ids_hbm, weight_hbm, cot_hbm, hid_hbm, *refs):
    same_ref, cross_ref, same_hid_ref, cross_hid_ref, ids_ref, weight_ref, cot_ref, hid_ref, sems = refs
    h = lax.axis_index("h")
    rows, half = same_ref.shape
    same = w_hbm.at[:, aligned(h, half, 128)]
    cross = w_hbm.at[:, aligned(1 - h, half, 128)]
    jobs = (
        (hid_hbm, hid_ref),
        (same, same_ref),
        (cross, cross_ref),
        (cross, cross_hid_ref.at[0:rows]),
        (same, same_hid_ref.at[0:rows]),
        (ids_hbm, ids_ref),
        (weight_hbm, weight_ref),
        (cot_hbm, cot_ref),
    )
    copies = [pltpu.make_async_copy(source, target, sems.at[i]) for i, (source, target) in enumerate(jobs)]
    for copy in copies:
        copy.start()
    copies[0].wait()
    packed = pack(hid_ref[...])
    same_hid_ref[rows:, 0 : packed.shape[1]] = packed
    cross_hid_ref[rows:, 0 : packed.shape[1]] = packed
    for copy in copies[1:]:
        copy.wait()


def route_body(experts, capacity, ids_ref, weight_ref, cot_ref, sent_ref, table_ref, index_ref):
    half = sent_ref.shape[1]
    ids = ids_ref[...]
    weights = weight_ref[...]
    tokens = ids.shape[1]
    row = lax.broadcasted_iota(jnp.int32, (tokens, tokens), 0)
    col = lax.broadcasted_iota(jnp.int32, (tokens, tokens), 1)
    earlier = jnp.where(row < col, 1.0, 0.0).astype(BF16)
    named = [jnp.sum(jnp.where(ids == e, 1.0, 0.0), axis=0, keepdims=True) for e in range(experts)]
    mixing = [jnp.sum(jnp.where(ids == e, weights, 0.0), axis=0, keepdims=True) for e in range(experts)]
    preceding = dot(jnp.concatenate(named, axis=0).astype(BF16), earlier, NN)
    slot = lax.broadcasted_iota(jnp.int32, (capacity, tokens), 0).astype(F32)
    chosen, combine = [], []
    index = jnp.full(ids.shape, -1.0, F32)
    for e in range(experts):
        rank = preceding[e : e + 1]
        match = jnp.where(rank == slot, 1.0, 0.0) * named[e]
        chosen.append(match)
        combine.append(match * mixing[e])
        index = jnp.where(ids == e, rank + float(e * capacity), index)
    index_ref[...] = index
    chosen = jnp.concatenate(chosen, axis=0)
    combine = jnp.concatenate(combine, axis=0)
    slots = chosen.shape[0]
    slot_weight = jnp.sum(combine, axis=1, keepdims=True)
    high = combine.astype(BF16)
    rest = combine - high.astype(F32)
    middle = rest.astype(BF16)
    table_ref[0:slots] = high
    table_ref[slots : 2 * slots] = middle
    table_ref[2 * slots : 3 * slots] = (rest - middle.astype(F32)).astype(BF16)
    gathered = dot(chosen.astype(BF16), cot_ref[...], NN)
    value = (gathered * slot_weight).astype(BF16)
    for g in range(2):
        sent_ref[g * slots : (g + 1) * slots] = value[:, g * half : (g + 1) * half]


def weight_grad_body(moves, groups, width, *refs):
    hidden_refs, (grad_ref, partner_ref, give_ref) = refs[:4], refs[4:7]
    sends, (hid_ref, total_ref) = refs[7 : 7 + len(moves)], refs[7 + len(moves) :]
    q, h, c = lax.axis_index("q"), lax.axis_index("h"), lax.axis_index("c")
    rows = sends[0].shape[0]
    slots = hid_ref.shape[0] // 4
    for ref, group in zip(hidden_refs, (h, 1 - h, 2 + h, 3 - h), strict=True):
        hid_ref[aligned(group, slots, 16), :] = unpack(ref[rows:], width)
    grads = jnp.concatenate([grad_ref[...], partner_ref[...]], axis=0)
    total_ref[...] = dot(hid_ref[...], grads, TN)
    for (dq, dh), send in zip(moves, sends, strict=True):
        target = (lax.rem(q + dq, groups) * 2 + lax.rem(h + dh, 2)) * 2 + c
        send[0:rows] = total_ref[aligned(target, rows, 8), :].astype(send.dtype)
    sends[1][rows:, 0 : 2 * width] = pack(give_ref[...])


def expert_body(moves, groups, width, *refs):
    count = len(moves)
    blocks = refs[: 2 * count]
    grad_ref, out_ref, keep_ref, give_ref, hid_ref, stage_ref = refs[2 * count :]
    q, h, c = lax.axis_index("q"), lax.axis_index("h"), lax.axis_index("c")
    slots = keep_ref.shape[0]
    rows = blocks[0].shape[0] - slots // 2
    for i, (dq, dh) in enumerate(moves):
        source = (lax.rem(q + (groups - dq), groups) * 2 + lax.rem(h + dh, 2)) * 2
        for side, core in ((0, c), (count, 1 - c)):
            stage_ref[aligned(source + core, rows, 8), :] = blocks[side + i][0:rows].astype(stage_ref.dtype)
    for i, group in enumerate((h, 1 - h)):
        hid_ref[aligned(group, slots, 16), :] = unpack(blocks[i][rows:], width)
    full = stage_ref[...].astype(BF16)
    out_ref[...] = dot(hid_ref[...], full, NN).astype(BF16)
    keep_ref[...] = dot(grad_ref[aligned(h, slots, 16), :], full, NT)
    give_ref[...] = dot(grad_ref[aligned(1 - h, slots, 16), :], full, NT).astype(BF16)


def combine_body(arrived_ref, table_ref, index_ref, cot_ref, layer_ref, route_ref):
    slots, half = arrived_ref.shape[0] // 2, arrived_ref.shape[1]
    scores = None
    for g in range(2):
        rows = arrived_ref[g * slots : (g + 1) * slots]
        mixed = dot(table_ref[...], jnp.concatenate([rows] * 3, axis=0), TN)
        layer_ref[:, g * half : (g + 1) * half] = mixed.astype(BF16)
        part = dot(rows, cot_ref[:, g * half : (g + 1) * half], NT)
        scores = part if scores is None else scores + part
    position = lax.broadcasted_iota(jnp.int32, scores.shape, 0).astype(F32)
    for k in range(index_ref.shape[0]):
        hit = position == index_ref[k : k + 1]
        route_ref[k : k + 1] = jnp.sum(jnp.where(hit, scores, 0.0), axis=0, keepdims=True)


def finish_body(moves, keep_ref, *refs):
    count = len(moves)
    terms, (hidden_ref, weight_ref) = refs[:count], refs[count:]
    h = lax.axis_index("h")
    rows, half = terms[0].shape
    given = unpack(terms[1][rows:], hidden_ref.shape[1])
    hidden_ref[...] = (keep_ref[...] + given.astype(F32)).astype(BF16)
    for side in range(2):
        total = None
        for (_, dh), term in zip(moves, terms, strict=True):
            if dh == side:
                value = term[0:rows].astype(F32)
                total = value if total is None else total + value
        weight_ref[:, aligned(h if side == 0 else 1 - h, half, 128)] = total


def local(route_ids, route_weights, hidden, down_weight, cotangent):
    groups = lax.axis_size("q")
    experts = lax.axis_size("ep")
    tokens, features = cotangent.shape
    capacity, width = hidden.shape[3], hidden.shape[4]
    rows = down_weight.shape[1]
    slots = experts * capacity
    choices = route_ids.shape[1]
    half = features // 2
    moves = [(0, 0), (0, 1)] + [(dq, dh) for dq in range(1, groups) for dh in range(2)]
    swap = [(0, 1), (1, 0)]

    def move(x, step):
        dq, dh = step
        pairs = [(a * 2 + b, (a + dq) % groups * 2 + (b + dh) % 2) for a in range(groups) for b in range(2)]
        return lax.ppermute(x, ("q", "h"), pairs)

    def swap_core(x):
        return lax.ppermute(x, "c", swap)

    def exchange(x):
        parts = x.reshape(2 * experts, capacity, half)
        return lax.all_to_all(parts, ("h", "ep"), split_axis=0, concat_axis=0, tiled=True).reshape(x.shape)

    plain = sds((rows, half), BF16)
    joined = sds((rows + slots // 2, half), BF16)
    parts = sds((2 * slots, half), BF16)
    same, cross, same_hid, cross_hid, ids, weights, cot = call(
        load_body,
        (plain, plain, joined, joined, sds((choices, tokens), route_ids.dtype), sds((choices, tokens), F32), sds(cotangent.shape, BF16)),
        [pltpu.VMEM((slots, width), BF16), pltpu.SemaphoreType.DMA((8,))],
        fetched=True,
        limit=LOAD_LIMIT,
    )(down_weight[0], route_ids.T, route_weights.T, cotangent, hidden.reshape(slots, width))

    blocks = [same_hid, move(cross_hid, moves[1])]
    blocks += [move(cross if step[1] else same, step) for i, step in enumerate(moves) if i > 1]
    blocks += [swap_core(b) for b in blocks]
    sent, table, index = call(
        functools.partial(route_body, experts, capacity),
        (parts, sds((3 * slots, tokens), BF16), sds((choices, tokens), F32)),
        flops=2 * slots * tokens * features,
    )(ids, weights, cot)
    grads = exchange(sent)
    partner_grads = swap_core(grads)

    given, keep, give = call(
        functools.partial(expert_body, moves, groups, width),
        (parts, sds((slots, width), F32), sds((slots, width), BF16)),
        [
            pltpu.VMEM((2 * slots, width), BF16),
            pltpu.VMEM((width, half), BF16 if rows % 16 == 0 else F32),
        ],
        flops=8 * slots * width * half,
    )(*blocks, grads)
    weight_terms = call(
        functools.partial(weight_grad_body, moves, groups, width),
        (sds((rows, half), F32), joined, *[plain] * (len(moves) - 2)),
        [pltpu.VMEM((4 * slots, width), BF16), pltpu.VMEM((width, half), F32)],
        flops=8 * slots * width * half,
    )(blocks[0], blocks[1], blocks[len(moves)], blocks[len(moves) + 1], grads, partner_grads, give)
    terms = [weight_terms[0]] + [move(weight_terms[i], step) for i, step in enumerate(moves) if i]

    arrived = exchange(given)

    layer_out, route_grad = call(
        combine_body, (sds((tokens, features), BF16), sds((choices, tokens), F32)), flops=8 * slots * tokens * features
    )(arrived, table, index, cot)

    hidden_grad, weight_grad = call(
        functools.partial(finish_body, moves),
        (sds((slots, width), BF16), sds((rows, features), F32)),
        flops=rows * features,
    )(keep, *terms)
    return layer_out, route_grad.T, hidden_grad.reshape(hidden.shape), weight_grad[None]


def solution(mesh):
    edp, ep = mesh.shape["edp"], mesh.shape["ep"]
    fine = Mesh(mesh.devices.reshape(edp // 4, 2, 2, ep), ("q", "h", "c", "ep"))
    group = ("q", "h", "c")
    tokens = P(group + ("ep",), None)
    slots = P(group, "ep", None, None, None)
    weights = P("ep", group, None)
    return jax.shard_map(
        local,
        mesh=fine,
        in_specs=(tokens, tokens, slots, weights, tokens),
        out_specs=(tokens, tokens, slots, weights),
        check_vma=False,
    )
```

time: 58.9 us -> 47.8 us (0.81)
  Pallas kernels: 15.3 us -> 6.35 us
  waiting for transfers between devices: 15.3 us -> 20.9 us
  local copies, waits for them, and re-layouts: 4.04 us -> 0 us
  starting transfers between devices: 22.9 us -> 19.5 us
    pallas_call x7 -> x6, Pallas kernels: 15.3 us -> 6.35 us  [run(): pl.pallas_call(body, out_shape=outs, in_specs=[inputs] * len(args), out_s...]
    unnamed x38 -> x0, local copies, waits for them, and re-layouts: 4.04 us -> none
    ppermute x9 -> x6, starting transfers between devices: 12.4 us -> 9.14 us  [move(): return lax.ppermute(x, ('q', 'h'), pairs)]
    ppermute x9 -> x6, waiting for transfers between devices: 15.3 us -> 18.1 us  [move(): return lax.ppermute(x, ('q', 'h'), pairs)]
    ppermute x6 -> x5, waiting for transfers between devices: 0.02 us -> 2.82 us  [swap_core(): return lax.ppermute(x, 'c', swap)]
  transfers between devices with their start and end apart: 17 -> 13, of which waited for: 6 -> 5; matrix products, arithmetic and copies ran while one was open for 0% -> 0% of each run, Pallas kernels for 19% -> 3%
where the time goes in v2:
time: 47.8 us; the launch traced here: 47.5 us
  waiting for transfers between devices  20.9 us (44%)
  starting transfers between devices  19.5 us (41%)
  Pallas kernels  6.35 us (13%)
  between operations  0.67 us (1%)
    ppermute x6, waiting for transfers between devices, move(): return lax.ppermute(x, ('q', 'h'), pairs)  18.1 us
    all_to_all x2, starting transfers between devices, exchange(): lax.all_to_all(parts, ('h', 'ep'), split_axis=0, concat_axis=0, tiled=True)  9.85 us
    ppermute x6, starting transfers between devices, move(): return lax.ppermute(x, ('q', 'h'), pairs)  9.14 us
    pallas_call x6, Pallas kernels, run(): pl.pallas_call(body, out_shape=outs, in_specs=[inputs] * len(args), out_s...  6.35 us
    ppermute x5, waiting for transfers between devices, swap_core(): return lax.ppermute(x, 'c', swap)  2.82 us
  transfers between devices with their start and end apart: 13, of which 5 were waited for; matrix products, arithmetic and copies ran while one was open for 0% of the time, Pallas kernels for 3%

profile of v2, /device:TPU:0, one launch (start us, length us, event | category | flops | bytes accessed | tf_op | source)
XLA Modules:
  0.0 47.5 jit_solution(2190851340042416158)
XLA Ops:
  0.6 1.4 %shard_map.84 = (bf16[48,1024]{1,0:T(8,128)(2,1)S(1)}, bf16[48,1024]{1,0:T(8,128)(2,1)S(1)}, bf16[80,1024]{1,0:T(8,128)(2,1)S(1)}, bf16[80,1024]{1,0:T(8,128)(2,...) custom-call(bf16[48,2048]{1,0:T(8,128)(2,1)} %bitcast.15, s32[8,128]{1,0:T(8,128)} %bitcast.17, ...), custom_call_target="tpu_custom_call" | custom-call | bytes 2113536 | tf_op jit(solution)/shard_map/pallas_call | solution.py:32
  2.0 1.1 %shard_map.85 = (bf16[128,1024]{1,0:T(8,128)(2,1)}, bf16[192,128]{1,0:T(8,128)(2,1)S(1)}, f32[8,128]{1,0:T(8,128)S(1)}) custom-call(s32[8,128]{1,0:T(8,128)S(1)} %get-tuple-element.29.ids_ref, f32[8,128]{1,0:T(8,128)S(1)} %get-tuple-element.30.weight_ref, bf16[128,2048]{1,0:T(8,128)(2,1)S(1)} %get-tuple-element.31.cot_ref), custom_call_target="tpu_custom_call" | custom-call | flops 33554432 | bytes 630784 | tf_op jit(solution)/shard_map/pallas_call | solution.py:32
  3.1 6.2 %all-to-all-start = ((bf16[8,16,1024]{2,1,0:T(8,128)(2,1)}), bf16[8,16,1024]{2,1,0:T(8,128)(2,1)S(1)}, u32[]{:S(2)}, u32[]{:S(2)}) async-start(bf16[8,16,1024]{2,1,0:T(8,128)(2,1)} %bitcast.4), calls=%async_computation | async-start | bytes 524288 | tf_op jit(solution)/shard_map/all_to_all | solution.py:214
  9.3 2.0 %collective-permute-start = (bf16[80,1024]{1,0:T(8,128)(2,1)S(1)}, bf16[80,1024]{1,0:T(8,128)(2,1)S(1)}, u32[]{:S(2)}, u32[]{:S(2)}) collective-permute-start(bf16[80,1024]{1,0:T(8,128)(2,1)S(1)} %get-tuple-element.26), channel_id=1, source_target_pairs={{0,8},{8,0},{16,24},{24,16},{1,9},{9,1},{17,25},{25,17},{2,10},{10... | collective-permute-start | bytes 491528 | tf_op jit(solution)/shard_map/ppermute | solution.py:207
  11.3 2.6 %collective-permute-start.1 = (bf16[48,1024]{1,0:T(8,128)(2,1)S(1)}, bf16[48,1024]{1,0:T(8,128)(2,1)S(1)}, u32[]{:S(2)}, u32[]{:S(2)}) collective-permute-start(bf16[48,1024]{1,0:T(8,128)(2,1)S(1)} %get-tuple-element.27), channel_id=1, source_target_pairs={{0,16},{8,24},{16,0},{24,8},{1,17},{9,25},{17,1},{25,9},{2,18},{10... | collective-permute-start | bytes 294920 | tf_op jit(solution)/shard_map/ppermute | solution.py:207
  13.9 0.0 collective-permute-start.2
  13.9 0.0 collective-permute-start.3
  13.9 6.2 %collective-permute-done.refs_1_ = bf16[80,1024]{1,0:T(8,128)(2,1)S(1)} collective-permute-done((bf16[80,1024]{1,0:T(8,128)(2,1)S(1)}, bf16[80,1024]{1,0:T(8,128)(2,1)S(1)}, u32[]{:S(2)}, u32[]{:S(2)}) %collective-permute-start) | collective-permute-done | bytes 163872 | tf_op jit(solution)/shard_map/ppermute | solution.py:207
  20.1 0.0 collective-permute-start.4
  20.1 0.0 collective-permute-done.1.refs_2_
  20.1 0.5 %collective-permute-start.5 = (bf16[48,1024]{1,0:T(8,128)(2,1)S(1)}, bf16[48,1024]{1,0:T(8,128)(2,1)S(1)}, u32[]{:S(2)}, u32[]{:S(2)}) collective-permute-start(bf16[48,1024]{1,0:T(8,128)(2,1)S(1)} %collective-permute-done.1.refs_2_), channel_id=1, source_target_pairs={{0,4},{4,0},{1,5},{5,1},{2,6},{6,2},{3,7},{7,3},{8,12},{12,8},{9,1... | collective-permute-start | bytes 294920 | tf_op jit(solution)/shard_map/ppermute | solution.py:210
  20.6 3.6 %collective-permute-done.2.refs_3_ = bf16[48,1024]{1,0:T(8,128)(2,1)S(1)} collective-permute-done((bf16[48,1024]{1,0:T(8,128)(2,1)S(1)}, bf16[48,1024]{1,0:T(8,128)(2,1)S(1)}, u32[]{:S(2)}, u32[]{:S(2)}) %collective-permute-start.2) | collective-permute-done | bytes 98336 | tf_op jit(solution)/shard_map/ppermute | solution.py:207
  24.2 0.0 collective-permute-start.6
  24.2 0.0 collective-permute-done.3.refs_4_.refs_2_
  24.2 0.0 collective-permute-done.5.refs_6_
  24.2 1.3 %collective-permute-done.6.refs_7_ = bf16[48,1024]{1,0:T(8,128)(2,1)S(1)} collective-permute-done((bf16[48,1024]{1,0:T(8,128)(2,1)S(1)}, bf16[48,1024]{1,0:T(8,128)(2,1)S(1)}, u32[]{:S(2)}, u32[]{:S(2)}) %collective-permute-start.6) | collective-permute-done | bytes 98336 | tf_op jit(solution)/shard_map/ppermute | solution.py:210
  25.5 0.0 collective-permute-done.4.refs_5_.refs_3_
  25.5 0.0 all-to-all-done
  25.5 1.4 %shard_map.86 = (bf16[128,1024]{1,0:T(8,128)(2,1)}, f32[64,384]{1,0:T(8,128)S(1)}, bf16[64,384]{1,0:T(8,128)(2,1)S(1)}) custom-call(bf16[80,1024]{1,0:T(8,128)(2,1)S(1)} %get-tuple-element.25.refs_0_, bf16[80,1024]{1,0:T(8,128)(2,1)S(1)} %collective-permute-done.refs_1_, bf16[48,1024]{1,0:T(8,128)(2,1)S(1)} %collective-permute-done.1.refs_2_, ...), custom_call_target="tpu_custom_call" | custom-call | flops 201326592 | bytes 819200 | tf_op jit(solution)/shard_map/pallas_call | solution.py:32
  26.9 3.6 %all-to-all-start.1 = ((bf16[8,16,1024]{2,1,0:T(8,128)(2,1)}), bf16[8,16,1024]{2,1,0:T(8,128)(2,1)S(1)}, u32[]{:S(2)}, u32[]{:S(2)}) async-start(bf16[8,16,1024]{2,1,0:T(8,128)(2,1)} %bitcast.6), calls=%async_computation.1 | async-start | bytes 524288 | tf_op jit(solution)/shard_map/all_to_all | solution.py:214
  30.5 0.0 collective-permute-start.7
  30.5 1.5 %collective-permute-done.7.refs_5_ = bf16[128,1024]{1,0:T(8,128)(2,1)S(1)} collective-permute-done((bf16[128,1024]{1,0:T(8,128)(2,1)S(1)}, bf16[128,1024]{1,0:T(8,128)(2,1)S(1)}, u32[]{:S(2)}, u32[]{:S(2)}) %collective-permute-start.7) | collective-permute-done | bytes 262176 | tf_op jit(solution)/shard_map/ppermute | solution.py:210
  32.1 0.5 shard_map.88
  32.5 2.1 %collective-permute-start.8 = (bf16[80,1024]{1,0:T(8,128)(2,1)S(1)}, bf16[80,1024]{1,0:T(8,128)(2,1)S(1)}, u32[]{:S(2)}, u32[]{:S(2)}) collective-permute-start(bf16[80,1024]{1,0:T(8,128)(2,1)S(1)} %get-tuple-element.41), channel_id=1, source_target_pairs={{0,8},{8,0},{16,24},{24,16},{1,9},{9,1},{17,25},{25,17},{2,10},{10... | collective-permute-start | bytes 491528 | tf_op jit(solution)/shard_map/ppermute | solution.py:207
  34.6 1.1 %collective-permute-start.9 = (bf16[48,1024]{1,0:T(8,128)(2,1)S(1)}, bf16[48,1024]{1,0:T(8,128)(2,1)S(1)}, u32[]{:S(2)}, u32[]{:S(2)}) collective-permute-start(bf16[48,1024]{1,0:T(8,128)(2,1)S(1)} %get-tuple-element.42), channel_id=1, source_target_pairs={{0,16},{8,24},{16,0},{24,8},{1,17},{9,25},{17,1},{25,9},{2,18},{10... | collective-permute-start | bytes 294920 | tf_op jit(solution)/shard_map/ppermute | solution.py:207
  35.7 1.4 %collective-permute-start.10 = (bf16[48,1024]{1,0:T(8,128)(2,1)S(1)}, bf16[48,1024]{1,0:T(8,128)(2,1)S(1)}, u32[]{:S(2)}, u32[]{:S(2)}) collective-permute-start(bf16[48,1024]{1,0:T(8,128)(2,1)S(1)} %get-tuple-element.43), channel_id=1, source_target_pairs={{0,24},{8,16},{16,8},{24,0},{1,25},{9,17},{17,9},{25,1},{2,26},{10... | collective-permute-start | bytes 294920 | tf_op jit(solution)/shard_map/ppermute | solution.py:207
  37.1 8.3 %collective-permute-done.9.refs_2_ = bf16[48,1024]{1,0:T(8,128)(2,1)S(1)} collective-permute-done((bf16[48,1024]{1,0:T(8,128)(2,1)S(1)}, bf16[48,1024]{1,0:T(8,128)(2,1)S(1)}, u32[]{:S(2)}, u32[]{:S(2)}) %collective-permute-start.9) | collective-permute-done | bytes 98336 | tf_op jit(solution)/shard_map/ppermute | solution.py:207
  45.4 0.0 collective-permute-done.10.refs_3_
  45.4 0.0 collective-permute-done.8.refs_1_
  45.4 0.8 %shard_map.89 = (bf16[64,384]{1,0:T(8,128)(2,1)}, f32[48,2048]{1,0:T(8,128)}) custom-call(f32[64,384]{1,0:T(8,128)S(1)} %get-tuple-element.38.keep_ref, f32[48,1024]{1,0:T(8,128)S(1)} %get-tuple-element.40.refs_0_, bf16[80,1024]{1,0:T(8,128)(2,1)S(1)} %collective-permute-done.8.refs_1_, bf16[48,1024]{1,0:T(8,128)(2,1)S(1)} %collective-permute-done.9.refs_2_, ...), custom_call_target="tpu_custom_call" | custom-call | flops 98304 | bytes 884736 | tf_op jit(solution)/shard_map/pallas_call | solution.py:32
  46.2 0.0 all-to-all-done.1
  46.2 1.2 %shard_map.87 = (bf16[128,2048]{1,0:T(8,128)(2,1)}, f32[8,128]{1,0:T(8,128)}) custom-call(bf16[128,1024]{1,0:T(8,128)(2,1)S(1)} %bitcast.14, bf16[192,128]{1,0:T(8,128)(2,1)S(1)} %get-tuple-element.34.table_ref, f32[8,128]{1,0:T(8,128)S(1)} %get-tuple-element.35.index_ref, bf16[128,2048]{1,0:T(8,128)(2,1)S(1)} %get-tuple-element.31.cot_ref), custom_call_target="tpu_custom_call" | custom-call | flops 134217728 | bytes 1056768 | tf_op jit(solution)/shard_map/pallas_call | solution.py:32
Async XLA Ops:
  3.1 22.4 %all-to-all-start = ((bf16[8,16,1024]{2,1,0:T(8,128)(2,1)}), bf16[8,16,1024]{2,1,0:T(8,128)(2,1)S(1)}, u32[]{:S(2)}, u32[]{:S(2)}) async-start(bf16[8,16,1024]{2,1,0:T(8,128)(2,1)} %bitcast.4), calls=%async_computation | async-start | bytes 524288 | tf_op jit(solution)/shard_map/all_to_all | solution.py:214
  9.3 10.8 %collective-permute-start = (bf16[80,1024]{1,0:T(8,128)(2,1)S(1)}, bf16[80,1024]{1,0:T(8,128)(2,1)S(1)}, u32[]{:S(2)}, u32[]{:S(2)}) collective-permute-start(bf16[80,1024]{1,0:T(8,128)(2,1)S(1)} %get-tuple-element.26), channel_id=1, source_target_pairs={{0,8},{8,0},{16,24},{24,16},{1,9},{9,1},{17,25},{25,17},{2,10},{10... | collective-permute-start | bytes 491528 | tf_op jit(solution)/shard_map/ppermute | solution.py:207
  11.3 8.8 %collective-permute-start.1 = (bf16[48,1024]{1,0:T(8,128)(2,1)S(1)}, bf16[48,1024]{1,0:T(8,128)(2,1)S(1)}, u32[]{:S(2)}, u32[]{:S(2)}) collective-permute-start(bf16[48,1024]{1,0:T(8,128)(2,1)S(1)} %get-tuple-element.27), channel_id=1, source_target_pairs={{0,16},{8,24},{16,0},{24,8},{1,17},{9,25},{17,1},{25,9},{2,18},{10... | collective-permute-start | bytes 294920 | tf_op jit(solution)/shard_map/ppermute | solution.py:207
  13.9 10.3 %collective-permute-start.2 = (bf16[48,1024]{1,0:T(8,128)(2,1)S(1)}, bf16[48,1024]{1,0:T(8,128)(2,1)S(1)}, u32[]{:S(2)}, u32[]{:S(2)}) collective-permute-start(bf16[48,1024]{1,0:T(8,128)(2,1)S(1)} %get-tuple-element.28), channel_id=1, source_target_pairs={{0,24},{8,16},{16,8},{24,0},{1,25},{9,17},{17,9},{25,1},{2,26},{10... | collective-permute-start | bytes 294920 | tf_op jit(solution)/shard_map/ppermute | solution.py:207
  13.9 10.3 %collective-permute-start.3 = (bf16[80,1024]{1,0:T(8,128)(2,1)S(1)}, bf16[80,1024]{1,0:T(8,128)(2,1)S(1)}, u32[]{:S(2)}, u32[]{:S(2)}) collective-permute-start(bf16[80,1024]{1,0:T(8,128)(2,1)S(1)} %get-tuple-element.25.refs_0_), channel_id=1, source_target_pairs={{0,4},{4,0},{1,5},{5,1},{2,6},{6,2},{3,7},{7,3},{8,12},{12,8},{9,1... | collective-permute-start | bytes 491528 | tf_op jit(solution)/shard_map/ppermute | solution.py:210
  20.1 5.4 %collective-permute-start.4 = (bf16[80,1024]{1,0:T(8,128)(2,1)S(1)}, bf16[80,1024]{1,0:T(8,128)(2,1)S(1)}, u32[]{:S(2)}, u32[]{:S(2)}) collective-permute-start(bf16[80,1024]{1,0:T(8,128)(2,1)S(1)} %collective-permute-done.refs_1_), channel_id=1, source_target_pairs={{0,4},{4,0},{1,5},{5,1},{2,6},{6,2},{3,7},{7,3},{8,12},{12,8},{9,1... | collective-permute-start | bytes 491528 | tf_op jit(solution)/shard_map/ppermute | solution.py:210
  20.1 4.1 %collective-permute-start.5 = (bf16[48,1024]{1,0:T(8,128)(2,1)S(1)}, bf16[48,1024]{1,0:T(8,128)(2,1)S(1)}, u32[]{:S(2)}, u32[]{:S(2)}) collective-permute-start(bf16[48,1024]{1,0:T(8,128)(2,1)S(1)} %collective-permute-done.1.refs_2_), channel_id=1, source_target_pairs={{0,4},{4,0},{1,5},{5,1},{2,6},{6,2},{3,7},{7,3},{8,12},{12,8},{9,1... | collective-permute-start | bytes 294920 | tf_op jit(solution)/shard_map/ppermute | solution.py:210
  24.2 1.3 %collective-permute-start.6 = (bf16[48,1024]{1,0:T(8,128)(2,1)S(1)}, bf16[48,1024]{1,0:T(8,128)(2,1)S(1)}, u32[]{:S(2)}, u32[]{:S(2)}) collective-permute-start(bf16[48,1024]{1,0:T(8,128)(2,1)S(1)} %collective-permute-done.2.refs_3_), channel_id=1, source_target_pairs={{0,4},{4,0},{1,5},{5,1},{2,6},{6,2},{3,7},{7,3},{8,12},{12,8},{9,1... | collective-permute-start | bytes 294920 | tf_op jit(solution)/shard_map/ppermute | solution.py:210
  26.9 19.3 %all-to-all-start.1 = ((bf16[8,16,1024]{2,1,0:T(8,128)(2,1)}), bf16[8,16,1024]{2,1,0:T(8,128)(2,1)S(1)}, u32[]{:S(2)}, u32[]{:S(2)}) async-start(bf16[8,16,1024]{2,1,0:T(8,128)(2,1)} %bitcast.6), calls=%async_computation.1 | async-start | bytes 524288 | tf_op jit(solution)/shard_map/all_to_all | solution.py:214
  30.5 1.5 %collective-permute-start.7 = (bf16[128,1024]{1,0:T(8,128)(2,1)S(1)}, bf16[128,1024]{1,0:T(8,128)(2,1)S(1)}, u32[]{:S(2)}, u32[]{:S(2)}) collective-permute-start(bf16[128,1024]{1,0:T(8,128)(2,1)S(1)} %bitcast.12), channel_id=1, source_target_pairs={{0,4},{4,0},{1,5},{5,1},{2,6},{6,2},{3,7},{7,3},{8,12},{12,8},{9,1... | collective-permute-start | bytes 786440 | tf_op jit(solution)/shard_map/ppermute | solution.py:210
  32.5 12.9 %collective-permute-start.8 = (bf16[80,1024]{1,0:T(8,128)(2,1)S(1)}, bf16[80,1024]{1,0:T(8,128)(2,1)S(1)}, u32[]{:S(2)}, u32[]{:S(2)}) collective-permute-start(bf16[80,1024]{1,0:T(8,128)(2,1)S(1)} %get-tuple-element.41), channel_id=1, source_target_pairs={{0,8},{8,0},{16,24},{24,16},{1,9},{9,1},{17,25},{25,17},{2,10},{10... | collective-permute-start | bytes 491528 | tf_op jit(solution)/shard_map/ppermute | solution.py:207
  34.6 10.8 %collective-permute-start.9 = (bf16[48,1024]{1,0:T(8,128)(2,1)S(1)}, bf16[48,1024]{1,0:T(8,128)(2,1)S(1)}, u32[]{:S(2)}, u32[]{:S(2)}) collective-permute-start(bf16[48,1024]{1,0:T(8,128)(2,1)S(1)} %get-tuple-element.42), channel_id=1, source_target_pairs={{0,16},{8,24},{16,0},{24,8},{1,17},{9,25},{17,1},{25,9},{2,18},{10... | collective-permute-start | bytes 294920 | tf_op jit(solution)/shard_map/ppermute | solution.py:207
  35.7 9.7 %collective-permute-start.10 = (bf16[48,1024]{1,0:T(8,128)(2,1)S(1)}, bf16[48,1024]{1,0:T(8,128)(2,1)S(1)}, u32[]{:S(2)}, u32[]{:S(2)}) collective-permute-start(bf16[48,1024]{1,0:T(8,128)(2,1)S(1)} %get-tuple-element.43), channel_id=1, source_target_pairs={{0,24},{8,16},{16,8},{24,0},{1,25},{9,17},{17,9},{25,1},{2,26},{10... | collective-permute-start | bytes 294920 | tf_op jit(solution)/shard_map/ppermute | solution.py:207

commit v3 on v2

--- a/solution.py
+++ b/solution.py
@@ -9,7 +9,6 @@
 from jax.sharding import PartitionSpec as P
 
 
-LOAD_LIMIT = 16 * 2**20
 BF16 = jnp.bfloat16
 F32 = jnp.float32
 NN = (((1,), (0,)), ((), ()))
@@ -86,10 +85,7 @@
         copy.wait()
 
 
-def route_body(experts, capacity, ids_ref, weight_ref, cot_ref, sent_ref, table_ref, index_ref):
-    half = sent_ref.shape[1]
-    ids = ids_ref[...]
-    weights = weight_ref[...]
+def slot_tables(experts, capacity, ids, weights):
     tokens = ids.shape[1]
     row = lax.broadcasted_iota(jnp.int32, (tokens, tokens), 0)
     col = lax.broadcasted_iota(jnp.int32, (tokens, tokens), 1)
@@ -98,29 +94,56 @@
     mixing = [jnp.sum(jnp.where(ids == e, weights, 0.0), axis=0, keepdims=True) for e in range(experts)]
     preceding = dot(jnp.concatenate(named, axis=0).astype(BF16), earlier, NN)
     slot = lax.broadcasted_iota(jnp.int32, (capacity, tokens), 0).astype(F32)
-    chosen, combine = [], []
+    chosen = [jnp.where(preceding[e : e + 1] == slot, 1.0, 0.0) * named[e] for e in range(experts)]
+    combine = jnp.concatenate([match * mix for match, mix in zip(chosen, mixing, strict=True)], axis=0)
+    return preceding, jnp.concatenate(chosen, axis=0), combine
+
+
+def route_body(experts, capacity, ids_ref, weight_ref, cot_ref, sent_ref):
+    half = sent_ref.shape[1]
+    _, chosen, combine = slot_tables(experts, capacity, ids_ref[...], weight_ref[...])
+    slots = chosen.shape[0]
+    slot_weight = jnp.sum(combine, axis=1, keepdims=True)
+    gathered = dot(chosen.astype(BF16), cot_ref[...], NN)
+    value = (gathered * slot_weight).astype(BF16)
+    for g in range(2):
+        sent_ref[g * slots : (g + 1) * slots] = value[:, g * half : (g + 1) * half]
+
+
+def tables_body(experts, capacity, ids_ref, weight_ref, table_ref, index_ref):
+    ids = ids_ref[...]
+    preceding, _, combine = slot_tables(experts, capacity, ids, weight_ref[...])
     index = jnp.full(ids.shape, -1.0, F32)
     for e in range(experts):
-        rank = preceding[e : e + 1]
-        match = jnp.where(rank == slot, 1.0, 0.0) * named[e]
-        chosen.append(match)
-        combine.append(match * mixing[e])
-        index = jnp.where(ids == e, rank + float(e * capacity), index)
+        index = jnp.where(ids == e, preceding[e : e + 1] + float(e * capacity), index)
     index_ref[...] = index
-    chosen = jnp.concatenate(chosen, axis=0)
-    combine = jnp.concatenate(combine, axis=0)
-    slots = chosen.shape[0]
-    slot_weight = jnp.sum(combine, axis=1, keepdims=True)
+    slots = combine.shape[0]
     high = combine.astype(BF16)
     rest = combine - high.astype(F32)
     middle = rest.astype(BF16)
     table_ref[0:slots] = high
     table_ref[slots : 2 * slots] = middle
     table_ref[2 * slots : 3 * slots] = (rest - middle.astype(F32)).astype(BF16)
-    gathered = dot(chosen.astype(BF16), cot_ref[...], NN)
-    value = (gathered * slot_weight).astype(BF16)
-    for g in range(2):
-        sent_ref[g * slots : (g + 1) * slots] = value[:, g * half : (g + 1) * half]
+
+
+def peer(index, step, count):
+    if count & (count - 1) == 0:
+        return index ^ step
+    return lax.rem(index + step, count)
+
+
+def origin(index, step, count):
+    return peer(index, step if count & (count - 1) == 0 else (count - step) % count, count)
+
+
+def join_body(own_ref, other_ref, *pieces):
+    h, s = lax.axis_index("h"), lax.axis_index("ep")
+    count = len(pieces)
+    unit = own_ref.shape[0] // count
+    for step, piece in enumerate(pieces):
+        rows = aligned(peer(s, step, count), unit, 16)
+        piece[aligned(h, unit, 16), :] = own_ref[rows, :]
+        piece[aligned(1 - h, unit, 16), :] = other_ref[rows, :]
 
 
 def weight_grad_body(moves, groups, width, *refs):
@@ -142,7 +165,7 @@
 def expert_body(moves, groups, width, *refs):
     count = len(moves)
     blocks = refs[: 2 * count]
-    grad_ref, out_ref, keep_ref, give_ref, hid_ref, stage_ref = refs[2 * count :]
+    grad_ref, own_ref, other_ref, keep_ref, give_ref, hid_ref, stage_ref = refs[2 * count :]
     q, h, c = lax.axis_index("q"), lax.axis_index("h"), lax.axis_index("c")
     slots = keep_ref.shape[0]
     rows = blocks[0].shape[0] - slots // 2
@@ -150,16 +173,26 @@
         source = (lax.rem(q + (groups - dq), groups) * 2 + lax.rem(h + dh, 2)) * 2
         for side, core in ((0, c), (count, 1 - c)):
             stage_ref[aligned(source + core, rows, 8), :] = blocks[side + i][0:rows].astype(stage_ref.dtype)
-    for i, group in enumerate((h, 1 - h)):
-        hid_ref[aligned(group, slots, 16), :] = unpack(blocks[i][rows:], width)
+    for i in range(2):
+        hid_ref[i * slots : (i + 1) * slots] = unpack(blocks[i][rows:], width)
     full = stage_ref[...].astype(BF16)
-    out_ref[...] = dot(hid_ref[...], full, NN).astype(BF16)
+    out = dot(hid_ref[...], full, NN).astype(BF16)
+    own_ref[...] = out[0:slots]
+    other_ref[...] = out[slots:]
     keep_ref[...] = dot(grad_ref[aligned(h, slots, 16), :], full, NT)
     give_ref[...] = dot(grad_ref[aligned(1 - h, slots, 16), :], full, NT).astype(BF16)
 
 
-def combine_body(arrived_ref, table_ref, index_ref, cot_ref, layer_ref, route_ref):
-    slots, half = arrived_ref.shape[0] // 2, arrived_ref.shape[1]
+def combine_body(table_ref, index_ref, cot_ref, *refs):
+    pieces, (layer_ref, route_ref, arrived_ref) = refs[:-3], refs[-3:]
+    count = len(pieces)
+    unit = pieces[0].shape[0] // 2
+    slots, half = count * unit, arrived_ref.shape[1]
+    s = lax.axis_index("ep")
+    for step, piece in enumerate(pieces):
+        source = origin(s, step, count)
+        for g in range(2):
+            arrived_ref[aligned(g * count + source, unit, 16), :] = piece[g * unit : (g + 1) * unit]
     scores = None
     for g in range(2):
         rows = arrived_ref[g * slots : (g + 1) * slots]
@@ -216,34 +249,39 @@
     plain = sds((rows, half), BF16)
     joined = sds((rows + slots // 2, half), BF16)
     parts = sds((2 * slots, half), BF16)
+    part = sds((slots, half), BF16)
     same, cross, same_hid, cross_hid, ids, weights, cot = call(
         load_body,
         (plain, plain, joined, joined, sds((choices, tokens), route_ids.dtype), sds((choices, tokens), F32), sds(cotangent.shape, BF16)),
         [pltpu.VMEM((slots, width), BF16), pltpu.SemaphoreType.DMA((8,))],
         fetched=True,
-        limit=LOAD_LIMIT,
     )(down_weight[0], route_ids.T, route_weights.T, cotangent, hidden.reshape(slots, width))
 
     blocks = [same_hid, move(cross_hid, moves[1])]
     blocks += [move(cross if step[1] else same, step) for i, step in enumerate(moves) if i > 1]
     blocks += [swap_core(b) for b in blocks]
-    sent, table, index = call(
-        functools.partial(route_body, experts, capacity),
-        (parts, sds((3 * slots, tokens), BF16), sds((choices, tokens), F32)),
-        flops=2 * slots * tokens * features,
+    sent = call(
+        functools.partial(route_body, experts, capacity), parts, flops=2 * slots * tokens * features
     )(ids, weights, cot)
+    table, index = call(
+        functools.partial(tables_body, experts, capacity),
+        (sds((3 * slots, tokens), BF16), sds((choices, tokens), F32)),
+        flops=2 * tokens * tokens * experts,
+    )(ids, weights)
     grads = exchange(sent)
     partner_grads = swap_core(grads)
 
-    given, keep, give = call(
+    own_out, other_out, keep, give = call(
         functools.partial(expert_body, moves, groups, width),
-        (parts, sds((slots, width), F32), sds((slots, width), BF16)),
+        (part, part, sds((slots, width), F32), sds((slots, width), BF16)),
         [
             pltpu.VMEM((2 * slots, width), BF16),
             pltpu.VMEM((width, half), BF16 if rows % 16 == 0 else F32),
         ],
         flops=8 * slots * width * half,
     )(*blocks, grads)
+    other_half = lax.ppermute(other_out, "h", swap)
+
     weight_terms = call(
         functools.partial(weight_grad_body, moves, groups, width),
         (sds((rows, half), F32), joined, *[plain] * (len(moves) - 2)),
@@ -252,11 +290,18 @@
     )(blocks[0], blocks[1], blocks[len(moves)], blocks[len(moves) + 1], grads, partner_grads, give)
     terms = [weight_terms[0]] + [move(weight_terms[i], step) for i, step in enumerate(moves) if i]
 
-    arrived = exchange(given)
+    parcels = call(join_body, (sds((2 * capacity, half), BF16),) * experts, flops=slots)(own_out, other_half)
+    arrived = [parcels[0]]
+    for step in range(1, experts):
+        pairs = [(e, int(peer(e, step, experts))) for e in range(experts)]
+        arrived.append(lax.ppermute(parcels[step], "ep", pairs))
 
     layer_out, route_grad = call(
-        combine_body, (sds((tokens, features), BF16), sds((choices, tokens), F32)), flops=8 * slots * tokens * features
-    )(arrived, table, index, cot)
+        combine_body,
+        (sds((tokens, features), BF16), sds((choices, tokens), F32)),
+        [pltpu.VMEM((2 * slots, half), BF16)],
+        flops=8 * slots * tokens * features,
+    )(table, index, cot, *arrived)
 
     hidden_grad, weight_grad = call(
         functools.partial(finish_body, moves),

time: 47.8 us -> 45.6 us (0.954)
  waiting for transfers between devices: 20.9 us -> 18.5 us
  starting transfers between devices: 19.5 us -> 20.2 us
    ppermute x6, waiting for transfers between devices: 18.1 us -> 9.71 us  [move(): return lax.ppermute(x, ('q', 'h'), pairs)]
    ppermute x0 -> x4, waiting for transfers between devices: none -> 7.48 us  [the longest x1 3.79 us: local(): other_half = lax.ppermute(other_out, 'h', swap)]
    ppermute x0 -> x4, starting transfers between devices: none -> 4.4 us  [the longest x3 4.33 us: local(): arrived.append(lax.ppermute(parcels[step], 'ep', pairs))]
    all_to_all x2 -> x1, starting transfers between devices: 9.85 us -> 6.21 us  [exchange(): lax.all_to_all(parts, ('h', 'ep'), split_axis=0, concat_axis=0, tiled=True)]
    ppermute x5, waiting for transfers between devices: 2.82 us -> 1.3 us  [swap_core(): return lax.ppermute(x, 'c', swap)]
    pallas_call x6 -> x8, Pallas kernels: 6.35 us -> 5.94 us  [run(): pl.pallas_call(body, out_shape=outs, in_specs=[inputs] * len(args), out_s...]
  transfers between devices with their start and end apart: 13 -> 16, of which waited for: 5 -> 6; matrix products, arithmetic and copies ran while one was open for 0% -> 0% of each run, Pallas kernels for 3% -> 6%
where the time goes in v3:
time: 45.6 us; the launch traced here: 45.4 us
  starting transfers between devices  20.2 us (44%)
  waiting for transfers between devices  18.5 us (41%)
  Pallas kernels  5.94 us (13%)
  between operations  0.7 us (2%)
    ppermute x6, waiting for transfers between devices, move(): return lax.ppermute(x, ('q', 'h'), pairs)  9.71 us
    ppermute x6, starting transfers between devices, move(): return lax.ppermute(x, ('q', 'h'), pairs)  9.05 us
    all_to_all x1, starting transfers between devices, exchange(): lax.all_to_all(parts, ('h', 'ep'), split_axis=0, concat_axis=0, tiled=True)  6.21 us
    pallas_call x8, Pallas kernels, run(): pl.pallas_call(body, out_shape=outs, in_specs=[inputs] * len(args), out_s...  5.94 us
    ppermute x3, starting transfers between devices, local(): arrived.append(lax.ppermute(parcels[step], 'ep', pairs))  4.33 us
    ppermute x1, waiting for transfers between devices, local(): other_half = lax.ppermute(other_out, 'h', swap)  3.79 us
    ppermute x3, waiting for transfers between devices, local(): arrived.append(lax.ppermute(parcels[step], 'ep', pairs))  3.69 us
    ppermute x5, waiting for transfers between devices, swap_core(): return lax.ppermute(x, 'c', swap)  1.3 us
  transfers between devices with their start and end apart: 16, of which 6 were waited for; matrix products, arithmetic and copies ran while one was open for 0% of the time, Pallas kernels for 6%

profile of v3, /device:TPU:0, one launch (start us, length us, event | category | flops | bytes accessed | tf_op | source)
XLA Modules:
  0.0 45.4 jit_solution(8244162959268805619)
XLA Ops:
  0.6 1.4 %shard_map.84 = (bf16[48,1024]{1,0:T(8,128)(2,1)S(1)}, bf16[48,1024]{1,0:T(8,128)(2,1)S(1)}, bf16[80,1024]{1,0:T(8,128)(2,1)S(1)}, bf16[80,1024]{1,0:T(8,128)(2,...) custom-call(bf16[48,2048]{1,0:T(8,128)(2,1)} %bitcast.12, s32[8,128]{1,0:T(8,128)} %bitcast.14, ...), custom_call_target="tpu_custom_call" | custom-call | bytes 2113536 | tf_op jit(solution)/shard_map/pallas_call | solution.py:31
  2.0 1.1 %shard_map.86 = bf16[128,1024]{1,0:T(8,128)(2,1)} custom-call(s32[8,128]{1,0:T(8,128)S(1)} %get-tuple-element.29.ids_ref, f32[8,128]{1,0:T(8,128)S(1)} %get-tuple-element.30.weight_ref, bf16[128,2048]{1,0:T(8,128)(2,1)S(1)} %get-tuple-element.33.cot_ref), custom_call_target="tpu_custom_call" | custom-call | flops 33554432 | bytes 524288 | tf_op jit(solution)/shard_map/pallas_call | solution.py:31
  3.1 6.2 %all-to-all-start = ((bf16[8,16,1024]{2,1,0:T(8,128)(2,1)}), bf16[8,16,1024]{2,1,0:T(8,128)(2,1)S(1)}, u32[]{:S(2)}, u32[]{:S(2)}) async-start(bf16[8,16,1024]{2,1,0:T(8,128)(2,1)} %bitcast.4), calls=%async_computation | async-start | bytes 524288 | tf_op jit(solution)/shard_map/all_to_all | solution.py:247
  9.3 2.0 %collective-permute-start = (bf16[80,1024]{1,0:T(8,128)(2,1)S(1)}, bf16[80,1024]{1,0:T(8,128)(2,1)S(1)}, u32[]{:S(2)}, u32[]{:S(2)}) collective-permute-start(bf16[80,1024]{1,0:T(8,128)(2,1)S(1)} %get-tuple-element.35), channel_id=1, source_target_pairs={{0,8},{8,0},{16,24},{24,16},{1,9},{9,1},{17,25},{25,17},{2,10},{10... | collective-permute-start | bytes 491528 | tf_op jit(solution)/shard_map/ppermute | solution.py:240
  11.3 2.6 %collective-permute-start.1 = (bf16[48,1024]{1,0:T(8,128)(2,1)S(1)}, bf16[48,1024]{1,0:T(8,128)(2,1)S(1)}, u32[]{:S(2)}, u32[]{:S(2)}) collective-permute-start(bf16[48,1024]{1,0:T(8,128)(2,1)S(1)} %get-tuple-element.36), channel_id=1, source_target_pairs={{0,16},{8,24},{16,0},{24,8},{1,17},{9,25},{17,1},{25,9},{2,18},{10... | collective-permute-start | bytes 294920 | tf_op jit(solution)/shard_map/ppermute | solution.py:240
  13.9 0.0 collective-permute-start.2
  13.9 0.0 collective-permute-start.3
  13.9 6.2 %collective-permute-done.refs_1_ = bf16[80,1024]{1,0:T(8,128)(2,1)S(1)} collective-permute-done((bf16[80,1024]{1,0:T(8,128)(2,1)S(1)}, bf16[80,1024]{1,0:T(8,128)(2,1)S(1)}, u32[]{:S(2)}, u32[]{:S(2)}) %collective-permute-start) | collective-permute-done | bytes 163872 | tf_op jit(solution)/shard_map/ppermute | solution.py:240
  20.1 0.0 collective-permute-start.4
  20.1 0.0 all-to-all-done
  20.1 0.5 %collective-permute-start.11 = (bf16[128,1024]{1,0:T(8,128)(2,1)S(1)}, bf16[128,1024]{1,0:T(8,128)(2,1)S(1)}, u32[]{:S(2)}, u32[]{:S(2)}) collective-permute-start(bf16[128,1024]{1,0:T(8,128)(2,1)S(1)} %bitcast.9), channel_id=1, source_target_pairs={{0,4},{4,0},{1,5},{5,1},{2,6},{6,2},{3,7},{7,3},{8,12},{12,8},{9,1... | collective-permute-start | bytes 786440 | tf_op jit(solution)/shard_map/ppermute | solution.py:243
  20.6 0.0 collective-permute-done.1.refs_2_
  20.6 0.1 collective-permute-start.5
  20.6 3.5 %collective-permute-done.2.refs_3_ = bf16[48,1024]{1,0:T(8,128)(2,1)S(1)} collective-permute-done((bf16[48,1024]{1,0:T(8,128)(2,1)S(1)}, bf16[48,1024]{1,0:T(8,128)(2,1)S(1)}, u32[]{:S(2)}, u32[]{:S(2)}) %collective-permute-start.2) | collective-permute-done | bytes 98336 | tf_op jit(solution)/shard_map/ppermute | solution.py:240
  24.2 0.0 collective-permute-start.6
  24.2 0.0 collective-permute-done.3.refs_4_.refs_2_
  24.2 0.0 collective-permute-done.5.refs_6_
  24.2 1.3 %collective-permute-done.6.refs_7_ = bf16[48,1024]{1,0:T(8,128)(2,1)S(1)} collective-permute-done((bf16[48,1024]{1,0:T(8,128)(2,1)S(1)}, bf16[48,1024]{1,0:T(8,128)(2,1)S(1)}, u32[]{:S(2)}, u32[]{:S(2)}) %collective-permute-start.6) | collective-permute-done | bytes 98336 | tf_op jit(solution)/shard_map/ppermute | solution.py:243
  25.5 0.0 collective-permute-done.4.refs_5_.refs_3_
  25.5 0.8 %shard_map.87 = (bf16[64,1024]{1,0:T(8,128)(2,1)S(1)}, bf16[64,1024]{1,0:T(8,128)(2,1)S(1)}, f32[64,384]{1,0:T(8,128)S(1)}, bf16[64,384]{1,0:T(8,128)(2,1)S(1)}) custom-call(bf16[80,1024]{1,0:T(8,128)(2,1)S(1)} %get-tuple-element.34.refs_0_, bf16[80,1024]{1,0:T(8,128)(2,1)S(1)} %collective-permute-done.refs_1_, ...), custom_call_target="tpu_custom_call" | custom-call | flops 201326592 | bytes 819200 | tf_op jit(solution)/shard_map/pallas_call | solution.py:31
  26.3 0.1 collective-permute-start.7
  26.4 0.0 collective-permute-done.11.refs_5_
  26.4 0.5 %shard_map.90 = (f32[48,1024]{1,0:T(8,128)S(1)}, bf16[80,1024]{1,0:T(8,128)(2,1)S(1)}, bf16[48,1024]{1,0:T(8,128)(2,1)S(1)}, bf16[48,1024]{1,0:T(8,128)(2,1)S(1)}) custom-call(bf16[80,1024]{1,0:T(8,128)(2,1)S(1)} %get-tuple-element.34.refs_0_, bf16[80,1024]{1,0:T(8,128)(2,1)S(1)} %collective-permute-done.refs_1_, ...), custom_call_target="tpu_custom_call" | custom-call | flops 201326592 | bytes 1114112 | tf_op jit(solution)/shard_map/pallas_call | solution.py:31
  26.9 2.1 %collective-permute-start.12 = (bf16[80,1024]{1,0:T(8,128)(2,1)S(1)}, bf16[80,1024]{1,0:T(8,128)(2,1)S(1)}, u32[]{:S(2)}, u32[]{:S(2)}) collective-permute-start(bf16[80,1024]{1,0:T(8,128)(2,1)S(1)} %get-tuple-element.49), channel_id=1, source_target_pairs={{0,8},{8,0},{16,24},{24,16},{1,9},{9,1},{17,25},{25,17},{2,10},{10... | collective-permute-start | bytes 491528 | tf_op jit(solution)/shard_map/ppermute | solution.py:240
  29.0 3.8 %collective-permute-done.7.other_ref = bf16[64,1024]{1,0:T(8,128)(2,1)S(1)} collective-permute-done((bf16[64,1024]{1,0:T(8,128)(2,1)S(1)}, bf16[64,1024]{1,0:T(8,128)(2,1)S(1)}, u32[]{:S(2)}, u32[]{:S(2)}) %collective-permute-start.7) | collective-permute-done | bytes 131104 | tf_op jit(solution)/shard_map/ppermute | solution.py:283
  32.8 1.5 %collective-permute-start.8 = (bf16[32,1024]{1,0:T(8,128)(2,1)S(1)}, bf16[32,1024]{1,0:T(8,128)(2,1)S(1)}, u32[]{:S(2)}, u32[]{:S(2)}) collective-permute-start(bf16[32,1024]{1,0:T(8,128)(2,1)S(1)} %get-tuple-element.41), channel_id=1, source_target_pairs={{0,1},{1,0},{2,3},{3,2},{4,5},{5,4},{6,7},{7,6},{8,9},{9,8},{10,11... | collective-permute-start | bytes 196616 | tf_op jit(solution)/shard_map/ppermute | solution.py:297
  34.3 0.0 collective-permute-start.13
  34.3 2.4 %collective-permute-start.14 = (bf16[48,1024]{1,0:T(8,128)(2,1)S(1)}, bf16[48,1024]{1,0:T(8,128)(2,1)S(1)}, u32[]{:S(2)}, u32[]{:S(2)}) collective-permute-start(bf16[48,1024]{1,0:T(8,128)(2,1)S(1)} %get-tuple-element.51), channel_id=1, source_target_pairs={{0,24},{8,16},{16,8},{24,0},{1,25},{9,17},{17,9},{25,1},{2,26},{10... | collective-permute-start | bytes 294920 | tf_op jit(solution)/shard_map/ppermute | solution.py:240
  36.7 1.5 %collective-permute-start.9 = (bf16[32,1024]{1,0:T(8,128)(2,1)S(1)}, bf16[32,1024]{1,0:T(8,128)(2,1)S(1)}, u32[]{:S(2)}, u32[]{:S(2)}) collective-permute-start(bf16[32,1024]{1,0:T(8,128)(2,1)S(1)} %get-tuple-element.42), channel_id=1, source_target_pairs={{0,2},{1,3},{2,0},{3,1},{4,6},{5,7},{6,4},{7,5},{8,10},{9,11},{10,... | collective-permute-start | bytes 196616 | tf_op jit(solution)/shard_map/ppermute | solution.py:297
  38.1 0.0 collective-permute-done.8.refs_1_
  38.1 1.3 %collective-permute-start.10 = (bf16[32,1024]{1,0:T(8,128)(2,1)S(1)}, bf16[32,1024]{1,0:T(8,128)(2,1)S(1)}, u32[]{:S(2)}, u32[]{:S(2)}) collective-permute-start(bf16[32,1024]{1,0:T(8,128)(2,1)S(1)} %get-tuple-element.43), channel_id=1, source_target_pairs={{0,3},{1,2},{2,1},{3,0},{4,7},{5,6},{6,5},{7,4},{8,11},{9,10},{10,... | collective-permute-start | bytes 196616 | tf_op jit(solution)/shard_map/ppermute | solution.py:297
  39.5 0.1 shard_map.85
  39.6 1.3 %collective-permute-done.9.refs_2_ = bf16[32,1024]{1,0:T(8,128)(2,1)S(1)} collective-permute-done((bf16[32,1024]{1,0:T(8,128)(2,1)S(1)}, bf16[32,1024]{1,0:T(8,128)(2,1)S(1)}, u32[]{:S(2)}, u32[]{:S(2)}) %collective-permute-start.9) | collective-permute-done | bytes 65568 | tf_op jit(solution)/shard_map/ppermute | solution.py:297
  41.0 2.4 %collective-permute-done.10.refs_3_ = bf16[32,1024]{1,0:T(8,128)(2,1)S(1)} collective-permute-done((bf16[32,1024]{1,0:T(8,128)(2,1)S(1)}, bf16[32,1024]{1,0:T(8,128)(2,1)S(1)}, u32[]{:S(2)}, u32[]{:S(2)}) %collective-permute-start.10) | collective-permute-done | bytes 65568 | tf_op jit(solution)/shard_map/ppermute | solution.py:297
  43.3 1.2 %shard_map.89 = (bf16[128,2048]{1,0:T(8,128)(2,1)}, f32[8,128]{1,0:T(8,128)}) custom-call(bf16[192,128]{1,0:T(8,128)(2,1)S(1)} %get-tuple-element.31.table_ref, f32[8,128]{1,0:T(8,128)S(1)} %get-tuple-element.32.index_ref, bf16[128,2048]{1,0:T(8,128)(2,1)S(1)} %get-tuple-element.33.cot_ref, bf16[32,1024]{1,0:T(8,128)(2,1)S(1)} %get-tuple-element.40.refs_0_, ...), custom_call_target="tpu_custom_call" | custom-call | flops 134217728 | bytes 1056768 | tf_op jit(solution)/shard_map/pallas_call | solution.py:31
  44.6 0.0 collective-permute-done.13.refs_2_
  44.6 0.0 collective-permute-done.14.refs_3_
  44.6 0.0 collective-permute-done.12.refs_1_
  44.6 0.8 %shard_map.91 = (bf16[64,384]{1,0:T(8,128)(2,1)}, f32[48,2048]{1,0:T(8,128)}) custom-call(f32[64,384]{1,0:T(8,128)S(1)} %get-tuple-element.46.keep_ref, f32[48,1024]{1,0:T(8,128)S(1)} %get-tuple-element.48.refs_0_, bf16[80,1024]{1,0:T(8,128)(2,1)S(1)} %collective-permute-done.12.refs_1_, bf16[48,1024]{1,0:T(8,128)(2,1)S(1)} %collective-permute-done.13.refs_2_, ...), custom_call_target="tpu_custom_call" | custom-call | flops 98304 | bytes 884736 | tf_op jit(solution)/shard_map/pallas_call | solution.py:31
  (1 shorter events, 0.0 us)
Async XLA Ops:
  3.1 17.0 %all-to-all-start = ((bf16[8,16,1024]{2,1,0:T(8,128)(2,1)}), bf16[8,16,1024]{2,1,0:T(8,128)(2,1)S(1)}, u32[]{:S(2)}, u32[]{:S(2)}) async-start(bf16[8,16,1024]{2,1,0:T(8,128)(2,1)} %bitcast.4), calls=%async_computation | async-start | bytes 524288 | tf_op jit(solution)/shard_map/all_to_all | solution.py:247
  9.3 10.8 %collective-permute-start = (bf16[80,1024]{1,0:T(8,128)(2,1)S(1)}, bf16[80,1024]{1,0:T(8,128)(2,1)S(1)}, u32[]{:S(2)}, u32[]{:S(2)}) collective-permute-start(bf16[80,1024]{1,0:T(8,128)(2,1)S(1)} %get-tuple-element.35), channel_id=1, source_target_pairs={{0,8},{8,0},{16,24},{24,16},{1,9},{9,1},{17,25},{25,17},{2,10},{10... | collective-permute-start | bytes 491528 | tf_op jit(solution)/shard_map/ppermute | solution.py:240
  11.3 9.3 %collective-permute-start.1 = (bf16[48,1024]{1,0:T(8,128)(2,1)S(1)}, bf16[48,1024]{1,0:T(8,128)(2,1)S(1)}, u32[]{:S(2)}, u32[]{:S(2)}) collective-permute-start(bf16[48,1024]{1,0:T(8,128)(2,1)S(1)} %get-tuple-element.36), channel_id=1, source_target_pairs={{0,16},{8,24},{16,0},{24,8},{1,17},{9,25},{17,1},{25,9},{2,18},{10... | collective-permute-start | bytes 294920 | tf_op jit(solution)/shard_map/ppermute | solution.py:240
  13.9 10.3 %collective-permute-start.2 = (bf16[48,1024]{1,0:T(8,128)(2,1)S(1)}, bf16[48,1024]{1,0:T(8,128)(2,1)S(1)}, u32[]{:S(2)}, u32[]{:S(2)}) collective-permute-start(bf16[48,1024]{1,0:T(8,128)(2,1)S(1)} %get-tuple-element.37), channel_id=1, source_target_pairs={{0,24},{8,16},{16,8},{24,0},{1,25},{9,17},{17,9},{25,1},{2,26},{10... | collective-permute-start | bytes 294920 | tf_op jit(solution)/shard_map/ppermute | solution.py:240
  13.9 10.3 %collective-permute-start.3 = (bf16[80,1024]{1,0:T(8,128)(2,1)S(1)}, bf16[80,1024]{1,0:T(8,128)(2,1)S(1)}, u32[]{:S(2)}, u32[]{:S(2)}) collective-permute-start(bf16[80,1024]{1,0:T(8,128)(2,1)S(1)} %get-tuple-element.34.refs_0_), channel_id=1, source_target_pairs={{0,4},{4,0},{1,5},{5,1},{2,6},{6,2},{3,7},{7,3},{8,12},{12,8},{9,1... | collective-permute-start | bytes 491528 | tf_op jit(solution)/shard_map/ppermute | solution.py:243
  20.1 5.4 %collective-permute-start.4 = (bf16[80,1024]{1,0:T(8,128)(2,1)S(1)}, bf16[80,1024]{1,0:T(8,128)(2,1)S(1)}, u32[]{:S(2)}, u32[]{:S(2)}) collective-permute-start(bf16[80,1024]{1,0:T(8,128)(2,1)S(1)} %collective-permute-done.refs_1_), channel_id=1, source_target_pairs={{0,4},{4,0},{1,5},{5,1},{2,6},{6,2},{3,7},{7,3},{8,12},{12,8},{9,1... | collective-permute-start | bytes 491528 | tf_op jit(solution)/shard_map/ppermute | solution.py:243
  20.1 6.3 %collective-permute-start.11 = (bf16[128,1024]{1,0:T(8,128)(2,1)S(1)}, bf16[128,1024]{1,0:T(8,128)(2,1)S(1)}, u32[]{:S(2)}, u32[]{:S(2)}) collective-permute-start(bf16[128,1024]{1,0:T(8,128)(2,1)S(1)} %bitcast.9), channel_id=1, source_target_pairs={{0,4},{4,0},{1,5},{5,1},{2,6},{6,2},{3,7},{7,3},{8,12},{12,8},{9,1... | collective-permute-start | bytes 786440 | tf_op jit(solution)/shard_map/ppermute | solution.py:243
  20.6 3.6 %collective-permute-start.5 = (bf16[48,1024]{1,0:T(8,128)(2,1)S(1)}, bf16[48,1024]{1,0:T(8,128)(2,1)S(1)}, u32[]{:S(2)}, u32[]{:S(2)}) collective-permute-start(bf16[48,1024]{1,0:T(8,128)(2,1)S(1)} %collective-permute-done.1.refs_2_), channel_id=1, source_target_pairs={{0,4},{4,0},{1,5},{5,1},{2,6},{6,2},{3,7},{7,3},{8,12},{12,8},{9,1... | collective-permute-start | bytes 294920 | tf_op jit(solution)/shard_map/ppermute | solution.py:243
  24.2 1.3 %collective-permute-start.6 = (bf16[48,1024]{1,0:T(8,128)(2,1)S(1)}, bf16[48,1024]{1,0:T(8,128)(2,1)S(1)}, u32[]{:S(2)}, u32[]{:S(2)}) collective-permute-start(bf16[48,1024]{1,0:T(8,128)(2,1)S(1)} %collective-permute-done.2.refs_3_), channel_id=1, source_target_pairs={{0,4},{4,0},{1,5},{5,1},{2,6},{6,2},{3,7},{7,3},{8,12},{12,8},{9,1... | collective-permute-start | bytes 294920 | tf_op jit(solution)/shard_map/ppermute | solution.py:243
  26.3 6.4 %collective-permute-start.7 = (bf16[64,1024]{1,0:T(8,128)(2,1)S(1)}, bf16[64,1024]{1,0:T(8,128)(2,1)S(1)}, u32[]{:S(2)}, u32[]{:S(2)}) collective-permute-start(bf16[64,1024]{1,0:T(8,128)(2,1)S(1)} %get-tuple-element.39), channel_id=1, source_target_pairs={{0,8},{8,0},{1,9},{9,1},{2,10},{10,2},{3,11},{11,3},{4,12},{12,4},... | collective-permute-start | bytes 393224 | tf_op jit(solution)/shard_map/ppermute | solution.py:283
  26.9 17.7 %collective-permute-start.12 = (bf16[80,1024]{1,0:T(8,128)(2,1)S(1)}, bf16[80,1024]{1,0:T(8,128)(2,1)S(1)}, u32[]{:S(2)}, u32[]{:S(2)}) collective-permute-start(bf16[80,1024]{1,0:T(8,128)(2,1)S(1)} %get-tuple-element.49), channel_id=1, source_target_pairs={{0,8},{8,0},{16,24},{24,16},{1,9},{9,1},{17,25},{25,17},{2,10},{10... | collective-permute-start | bytes 491528 | tf_op jit(solution)/shard_map/ppermute | solution.py:240
  32.8 5.4 %collective-permute-start.8 = (bf16[32,1024]{1,0:T(8,128)(2,1)S(1)}, bf16[32,1024]{1,0:T(8,128)(2,1)S(1)}, u32[]{:S(2)}, u32[]{:S(2)}) collective-permute-start(bf16[32,1024]{1,0:T(8,128)(2,1)S(1)} %get-tuple-element.41), channel_id=1, source_target_pairs={{0,1},{1,0},{2,3},{3,2},{4,5},{5,4},{6,7},{7,6},{8,9},{9,8},{10,11... | collective-permute-start | bytes 196616 | tf_op jit(solution)/shard_map/ppermute | solution.py:297
  34.3 10.2 %collective-permute-start.13 = (bf16[48,1024]{1,0:T(8,128)(2,1)S(1)}, bf16[48,1024]{1,0:T(8,128)(2,1)S(1)}, u32[]{:S(2)}, u32[]{:S(2)}) collective-permute-start(bf16[48,1024]{1,0:T(8,128)(2,1)S(1)} %get-tuple-element.50), channel_id=1, source_target_pairs={{0,16},{8,24},{16,0},{24,8},{1,17},{9,25},{17,1},{25,9},{2,18},{10... | collective-permute-start | bytes 294920 | tf_op jit(solution)/shard_map/ppermute | solution.py:240
  34.3 10.2 %collective-permute-start.14 = (bf16[48,1024]{1,0:T(8,128)(2,1)S(1)}, bf16[48,1024]{1,0:T(8,128)(2,1)S(1)}, u32[]{:S(2)}, u32[]{:S(2)}) collective-permute-start(bf16[48,1024]{1,0:T(8,128)(2,1)S(1)} %get-tuple-element.51), channel_id=1, source_target_pairs={{0,24},{8,16},{16,8},{24,0},{1,25},{9,17},{17,9},{25,1},{2,26},{10... | collective-permute-start | bytes 294920 | tf_op jit(solution)/shard_map/ppermute | solution.py:240
  36.7 4.3 %collective-permute-start.9 = (bf16[32,1024]{1,0:T(8,128)(2,1)S(1)}, bf16[32,1024]{1,0:T(8,128)(2,1)S(1)}, u32[]{:S(2)}, u32[]{:S(2)}) collective-permute-start(bf16[32,1024]{1,0:T(8,128)(2,1)S(1)} %get-tuple-element.42), channel_id=1, source_target_pairs={{0,2},{1,3},{2,0},{3,1},{4,6},{5,7},{6,4},{7,5},{8,10},{9,11},{10,... | collective-permute-start | bytes 196616 | tf_op jit(solution)/shard_map/ppermute | solution.py:297
  38.1 5.2 %collective-permute-start.10 = (bf16[32,1024]{1,0:T(8,128)(2,1)S(1)}, bf16[32,1024]{1,0:T(8,128)(2,1)S(1)}, u32[]{:S(2)}, u32[]{:S(2)}) collective-permute-start(bf16[32,1024]{1,0:T(8,128)(2,1)S(1)} %get-tuple-element.43), channel_id=1, source_target_pairs={{0,3},{1,2},{2,1},{3,0},{4,7},{5,6},{6,5},{7,4},{8,11},{9,10},{10,... | collective-permute-start | bytes 196616 | tf_op jit(solution)/shard_map/ppermute | solution.py:297

commit v4 on v3

--- a/solution.py
+++ b/solution.py
@@ -20,10 +20,11 @@
     return lax.dot_general(a, b, dims, preferred_element_type=F32)
 
 
-def call(body, outs, scratch=(), flops=0, fetched=False, limit=16 * 2**20):
+def call(body, outs, scratch=(), flops=0, fetched=False, written=False, limit=16 * 2**20):
     size = sum(o.size * o.dtype.itemsize for o in jax.tree.leaves(outs))
     space = pl.BlockSpec(memory_space=pltpu.VMEM)
     inputs = pl.BlockSpec(memory_space=pltpu.HBM) if fetched else space
+    outputs = pl.BlockSpec(memory_space=pltpu.HBM) if written else space
 
     def run(*args):
         if fetched:
@@ -32,7 +33,7 @@
             body,
             out_shape=outs,
             in_specs=[inputs] * len(args),
-            out_specs=jax.tree.map(lambda _: space, outs),
+            out_specs=jax.tree.map(lambda _: outputs, outs),
             scratch_shapes=scratch,
             compiler_params=pltpu.CompilerParams(vmem_limit_bytes=limit),
             cost_estimate=pl.CostEstimate(flops=flops, bytes_accessed=2 * size, transcendentals=0),
@@ -183,36 +184,18 @@
     give_ref[...] = dot(grad_ref[aligned(1 - h, slots, 16), :], full, NT).astype(BF16)
 
 
-def combine_body(table_ref, index_ref, cot_ref, *refs):
-    pieces, (layer_ref, route_ref, arrived_ref) = refs[:-3], refs[-3:]
-    count = len(pieces)
-    unit = pieces[0].shape[0] // 2
-    slots, half = count * unit, arrived_ref.shape[1]
-    s = lax.axis_index("ep")
-    for step, piece in enumerate(pieces):
-        source = origin(s, step, count)
-        for g in range(2):
-            arrived_ref[aligned(g * count + source, unit, 16), :] = piece[g * unit : (g + 1) * unit]
-    scores = None
-    for g in range(2):
-        rows = arrived_ref[g * slots : (g + 1) * slots]
-        mixed = dot(table_ref[...], jnp.concatenate([rows] * 3, axis=0), TN)
-        layer_ref[:, g * half : (g + 1) * half] = mixed.astype(BF16)
-        part = dot(rows, cot_ref[:, g * half : (g + 1) * half], NT)
-        scores = part if scores is None else scores + part
-    position = lax.broadcasted_iota(jnp.int32, scores.shape, 0).astype(F32)
-    for k in range(index_ref.shape[0]):
-        hit = position == index_ref[k : k + 1]
-        route_ref[k : k + 1] = jnp.sum(jnp.where(hit, scores, 0.0), axis=0, keepdims=True)
-
-
-def finish_body(moves, keep_ref, *refs):
+def finish_body(moves, experts, keep_ref, table_ref, index_ref, cot_ref, *refs):
     count = len(moves)
-    terms, (hidden_ref, weight_ref) = refs[:count], refs[count:]
-    h = lax.axis_index("h")
+    terms, pieces = refs[:count], refs[count : count + experts]
+    layer_hbm, route_hbm, hidden_hbm, weight_hbm, layer_ref, route_ref, hidden_ref, weight_ref, arrived_ref, sems = refs[count + experts :]
+    h, s = lax.axis_index("h"), lax.axis_index("ep")
     rows, half = terms[0].shape
-    given = unpack(terms[1][rows:], hidden_ref.shape[1])
-    hidden_ref[...] = (keep_ref[...] + given.astype(F32)).astype(BF16)
+    copies = []
+
+    def put(source, target):
+        copies.append(pltpu.make_async_copy(source, target, sems.at[len(copies)]))
+        copies[-1].start()
+
     for side in range(2):
         total = None
         for (_, dh), term in zip(moves, terms, strict=True):
@@ -220,6 +203,31 @@
                 value = term[0:rows].astype(F32)
                 total = value if total is None else total + value
         weight_ref[:, aligned(h if side == 0 else 1 - h, half, 128)] = total
+    put(weight_ref, weight_hbm)
+    given = unpack(terms[1][rows:], hidden_ref.shape[1])
+    hidden_ref[...] = (keep_ref[...] + given.astype(F32)).astype(BF16)
+    put(hidden_ref, hidden_hbm)
+    unit = pieces[0].shape[0] // 2
+    slots = experts * unit
+    for step, piece in enumerate(pieces):
+        source = origin(s, step, experts)
+        for g in range(2):
+            arrived_ref[aligned(g * experts + source, unit, 16), :] = piece[g * unit : (g + 1) * unit]
+    scores = None
+    for g in range(2):
+        block = arrived_ref[g * slots : (g + 1) * slots]
+        mixed = dot(table_ref[...], jnp.concatenate([block] * 3, axis=0), TN)
+        layer_ref[g] = mixed.astype(BF16)
+        put(layer_ref.at[g], layer_hbm.at[:, pl.ds(g * half, half)])
+        part = dot(block, cot_ref[:, g * half : (g + 1) * half], NT)
+        scores = part if scores is None else scores + part
+    position = lax.broadcasted_iota(jnp.int32, scores.shape, 0).astype(F32)
+    for k in range(index_ref.shape[0]):
+        hit = position == index_ref[k : k + 1]
+        route_ref[k : k + 1] = jnp.sum(jnp.where(hit, scores, 0.0), axis=0, keepdims=True)
+    put(route_ref, route_hbm)
+    for copy in copies:
+        copy.wait()
 
 
 def local(route_ids, route_weights, hidden, down_weight, cotangent):
@@ -296,18 +304,26 @@
         pairs = [(e, int(peer(e, step, experts))) for e in range(experts)]
         arrived.append(lax.ppermute(parcels[step], "ep", pairs))
 
-    layer_out, route_grad = call(
-        combine_body,
-        (sds((tokens, features), BF16), sds((choices, tokens), F32)),
-        [pltpu.VMEM((2 * slots, half), BF16)],
+    outs = (
+        sds((tokens, features), BF16),
+        sds((choices, tokens), F32),
+        sds((slots, width), BF16),
+        sds((rows, features), F32),
+    )
+    layer_out, route_grad, hidden_grad, weight_grad = call(
+        functools.partial(finish_body, moves, experts),
+        outs,
+        [
+            pltpu.VMEM((2, tokens, half), BF16),
+            pltpu.VMEM((choices, tokens), F32),
+            pltpu.VMEM((slots, width), BF16),
+            pltpu.VMEM((rows, features), F32),
+            pltpu.VMEM((2 * slots, half), BF16),
+            pltpu.SemaphoreType.DMA((5,)),
+        ],
         flops=8 * slots * tokens * features,
-    )(table, index, cot, *arrived)
-
-    hidden_grad, weight_grad = call(
-        functools.partial(finish_body, moves),
-        (sds((slots, width), BF16), sds((rows, features), F32)),
-        flops=rows * features,
-    )(keep, *terms)
+        written=True,
+    )(keep, table, index, cot, *terms, *arrived)
     return layer_out, route_grad.T, hidden_grad.reshape(hidden.shape), weight_grad[None]
 
 

time: 45.6 us -> 45.8 us (level)
  waiting for transfers between devices: 18.5 us -> 19.5 us
  Pallas kernels: 5.94 us -> 5.2 us
    ppermute x6, waiting for transfers between devices: 9.71 us -> 11.6 us  [move(): return lax.ppermute(x, ('q', 'h'), pairs)]
    ppermute x6, starting transfers between devices: 9.05 us -> 8.15 us  [move(): return lax.ppermute(x, ('q', 'h'), pairs)]
    ppermute x3, starting transfers between devices: 4.33 us -> 5.23 us  [local(): arrived.append(lax.ppermute(parcels[step], 'ep', pairs))]
    ppermute x3, waiting for transfers between devices: 3.69 us -> 2.79 us  [local(): arrived.append(lax.ppermute(parcels[step], 'ep', pairs))]
    pallas_call x8 -> x7, Pallas kernels: 5.94 us -> 5.2 us  [run(): pl.pallas_call(body, out_shape=outs, in_specs=[inputs] * len(args), out_s...]
  transfers between devices with their start and end apart: 16 -> 16, of which waited for: 6 -> 7; matrix products, arithmetic and copies ran while one was open for 0% -> 0% of each run, Pallas kernels for 6% -> 3%
where the time goes in v4:
time: 45.8 us; the launch traced here: 45.6 us
  starting transfers between devices  20.2 us (44%)
  waiting for transfers between devices  19.5 us (43%)
  Pallas kernels  5.2 us (11%)
  between operations  0.7 us (2%)
    ppermute x6, waiting for transfers between devices, move(): return lax.ppermute(x, ('q', 'h'), pairs)  11.6 us
    ppermute x6, starting transfers between devices, move(): return lax.ppermute(x, ('q', 'h'), pairs)  8.15 us
    all_to_all x1, starting transfers between devices, exchange(): lax.all_to_all(parts, ('h', 'ep'), split_axis=0, concat_axis=0, tiled=True)  6.21 us
    ppermute x3, starting transfers between devices, local(): arrived.append(lax.ppermute(parcels[step], 'ep', pairs))  5.23 us
    pallas_call x7, Pallas kernels, run(): pl.pallas_call(body, out_shape=outs, in_specs=[inputs] * len(args), out_s...  5.2 us
    ppermute x1, waiting for transfers between devices, local(): other_half = lax.ppermute(other_out, 'h', swap)  3.79 us
    ppermute x3, waiting for transfers between devices, local(): arrived.append(lax.ppermute(parcels[step], 'ep', pairs))  2.79 us
    ppermute x5, waiting for transfers between devices, swap_core(): return lax.ppermute(x, 'c', swap)  1.3 us
  transfers between devices with their start and end apart: 16, of which 7 were waited for; matrix products, arithmetic and copies ran while one was open for 0% of the time, Pallas kernels for 3%

profile of v4, /device:TPU:0, one launch (start us, length us, event | category | flops | bytes accessed | tf_op | source)
XLA Modules:
  0.0 45.6 jit_solution(10782820936004376029)
XLA Ops:
  0.6 1.4 %shard_map.84 = (bf16[48,1024]{1,0:T(8,128)(2,1)S(1)}, bf16[48,1024]{1,0:T(8,128)(2,1)S(1)}, bf16[80,1024]{1,0:T(8,128)(2,1)S(1)}, bf16[80,1024]{1,0:T(8,128)(2,...) custom-call(bf16[48,2048]{1,0:T(8,128)(2,1)} %bitcast.12, s32[8,128]{1,0:T(8,128)} %bitcast.14, ...), custom_call_target="tpu_custom_call" | custom-call | bytes 2113536 | tf_op jit(solution)/shard_map/pallas_call | solution.py:32
  2.0 1.1 %shard_map.85 = bf16[128,1024]{1,0:T(8,128)(2,1)} custom-call(s32[8,128]{1,0:T(8,128)S(1)} %get-tuple-element.33.ids_ref, f32[8,128]{1,0:T(8,128)S(1)} %get-tuple-element.34.weight_ref, bf16[128,2048]{1,0:T(8,128)(2,1)S(1)} %get-tuple-element.35.cot_ref), custom_call_target="tpu_custom_call" | custom-call | flops 33554432 | bytes 524288 | tf_op jit(solution)/shard_map/pallas_call | solution.py:32
  3.1 6.2 %all-to-all-start = ((bf16[8,16,1024]{2,1,0:T(8,128)(2,1)}), bf16[8,16,1024]{2,1,0:T(8,128)(2,1)S(1)}, u32[]{:S(2)}, u32[]{:S(2)}) async-start(bf16[8,16,1024]{2,1,0:T(8,128)(2,1)} %bitcast.4), calls=%async_computation | async-start | bytes 524288 | tf_op jit(solution)/shard_map/all_to_all | solution.py:255
  9.3 2.0 %collective-permute-start = (bf16[80,1024]{1,0:T(8,128)(2,1)S(1)}, bf16[80,1024]{1,0:T(8,128)(2,1)S(1)}, u32[]{:S(2)}, u32[]{:S(2)}) collective-permute-start(bf16[80,1024]{1,0:T(8,128)(2,1)S(1)} %get-tuple-element.30), channel_id=1, source_target_pairs={{0,8},{8,0},{16,24},{24,16},{1,9},{9,1},{17,25},{25,17},{2,10},{10... | collective-permute-start | bytes 491528 | tf_op jit(solution)/shard_map/ppermute | solution.py:248
  11.3 2.6 %collective-permute-start.1 = (bf16[48,1024]{1,0:T(8,128)(2,1)S(1)}, bf16[48,1024]{1,0:T(8,128)(2,1)S(1)}, u32[]{:S(2)}, u32[]{:S(2)}) collective-permute-start(bf16[48,1024]{1,0:T(8,128)(2,1)S(1)} %get-tuple-element.31), channel_id=1, source_target_pairs={{0,16},{8,24},{16,0},{24,8},{1,17},{9,25},{17,1},{25,9},{2,18},{10... | collective-permute-start | bytes 294920 | tf_op jit(solution)/shard_map/ppermute | solution.py:248
  13.9 0.0 collective-permute-start.2
  13.9 0.0 collective-permute-start.3
  13.9 6.2 %collective-permute-done.refs_1_ = bf16[80,1024]{1,0:T(8,128)(2,1)S(1)} collective-permute-done((bf16[80,1024]{1,0:T(8,128)(2,1)S(1)}, bf16[80,1024]{1,0:T(8,128)(2,1)S(1)}, u32[]{:S(2)}, u32[]{:S(2)}) %collective-permute-start) | collective-permute-done | bytes 163872 | tf_op jit(solution)/shard_map/ppermute | solution.py:248
  20.1 0.0 collective-permute-start.4
  20.1 0.0 all-to-all-done
  20.1 0.5 %collective-permute-start.7 = (bf16[128,1024]{1,0:T(8,128)(2,1)S(1)}, bf16[128,1024]{1,0:T(8,128)(2,1)S(1)}, u32[]{:S(2)}, u32[]{:S(2)}) collective-permute-start(bf16[128,1024]{1,0:T(8,128)(2,1)S(1)} %bitcast.9), channel_id=1, source_target_pairs={{0,4},{4,0},{1,5},{5,1},{2,6},{6,2},{3,7},{7,3},{8,12},{12,8},{9,1... | collective-permute-start | bytes 786440 | tf_op jit(solution)/shard_map/ppermute | solution.py:251
  20.6 0.0 collective-permute-done.1.refs_2_
  20.6 0.1 collective-permute-start.5
  20.6 3.5 %collective-permute-done.2.refs_3_ = bf16[48,1024]{1,0:T(8,128)(2,1)S(1)} collective-permute-done((bf16[48,1024]{1,0:T(8,128)(2,1)S(1)}, bf16[48,1024]{1,0:T(8,128)(2,1)S(1)}, u32[]{:S(2)}, u32[]{:S(2)}) %collective-permute-start.2) | collective-permute-done | bytes 98336 | tf_op jit(solution)/shard_map/ppermute | solution.py:248
  24.2 0.0 collective-permute-start.6
  24.2 0.0 collective-permute-done.3.refs_4_.refs_2_
  24.2 0.0 collective-permute-done.5.refs_6_
  24.2 1.3 %collective-permute-done.6.refs_7_ = bf16[48,1024]{1,0:T(8,128)(2,1)S(1)} collective-permute-done((bf16[48,1024]{1,0:T(8,128)(2,1)S(1)}, bf16[48,1024]{1,0:T(8,128)(2,1)S(1)}, u32[]{:S(2)}, u32[]{:S(2)}) %collective-permute-start.6) | collective-permute-done | bytes 98336 | tf_op jit(solution)/shard_map/ppermute | solution.py:251
  25.5 0.0 collective-permute-done.4.refs_5_.refs_3_
  25.5 0.8 %shard_map.86 = (bf16[64,1024]{1,0:T(8,128)(2,1)S(1)}, bf16[64,1024]{1,0:T(8,128)(2,1)S(1)}, f32[64,384]{1,0:T(8,128)S(1)}, bf16[64,384]{1,0:T(8,128)(2,1)S(1)}) custom-call(bf16[80,1024]{1,0:T(8,128)(2,1)S(1)} %get-tuple-element.29.refs_0_, bf16[80,1024]{1,0:T(8,128)(2,1)S(1)} %collective-permute-done.refs_1_, ...), custom_call_target="tpu_custom_call" | custom-call | flops 201326592 | bytes 819200 | tf_op jit(solution)/shard_map/pallas_call | solution.py:32
  26.3 0.1 collective-permute-start.11
  26.4 0.0 collective-permute-done.7.refs_5_
  26.4 0.5 %shard_map.88 = (f32[48,1024]{1,0:T(8,128)S(1)}, bf16[80,1024]{1,0:T(8,128)(2,1)S(1)}, bf16[48,1024]{1,0:T(8,128)(2,1)S(1)}, bf16[48,1024]{1,0:T(8,128)(2,1)S(1)}) custom-call(bf16[80,1024]{1,0:T(8,128)(2,1)S(1)} %get-tuple-element.29.refs_0_, bf16[80,1024]{1,0:T(8,128)(2,1)S(1)} %collective-permute-done.refs_1_, ...), custom_call_target="tpu_custom_call" | custom-call | flops 201326592 | bytes 1114112 | tf_op jit(solution)/shard_map/pallas_call | solution.py:32
  26.9 2.1 %collective-permute-start.8 = (bf16[80,1024]{1,0:T(8,128)(2,1)S(1)}, bf16[80,1024]{1,0:T(8,128)(2,1)S(1)}, u32[]{:S(2)}, u32[]{:S(2)}) collective-permute-start(bf16[80,1024]{1,0:T(8,128)(2,1)S(1)} %get-tuple-element.41), channel_id=1, source_target_pairs={{0,8},{8,0},{16,24},{24,16},{1,9},{9,1},{17,25},{25,17},{2,10},{10... | collective-permute-start | bytes 491528 | tf_op jit(solution)/shard_map/ppermute | solution.py:248
  29.0 3.8 %collective-permute-done.11.other_ref = bf16[64,1024]{1,0:T(8,128)(2,1)S(1)} collective-permute-done((bf16[64,1024]{1,0:T(8,128)(2,1)S(1)}, bf16[64,1024]{1,0:T(8,128)(2,1)S(1)}, u32[]{:S(2)}, u32[]{:S(2)}) %collective-permute-start.11) | collective-permute-done | bytes 131104 | tf_op jit(solution)/shard_map/ppermute | solution.py:291
  32.8 1.5 %collective-permute-start.12 = (bf16[32,1024]{1,0:T(8,128)(2,1)S(1)}, bf16[32,1024]{1,0:T(8,128)(2,1)S(1)}, u32[]{:S(2)}, u32[]{:S(2)}) collective-permute-start(bf16[32,1024]{1,0:T(8,128)(2,1)S(1)} %get-tuple-element.47), channel_id=1, source_target_pairs={{0,1},{1,0},{2,3},{3,2},{4,5},{5,4},{6,7},{7,6},{8,9},{9,8},{10,11... | collective-permute-start | bytes 196616 | tf_op jit(solution)/shard_map/ppermute | solution.py:305
  34.3 1.3 %collective-permute-start.10 = (bf16[48,1024]{1,0:T(8,128)(2,1)S(1)}, bf16[48,1024]{1,0:T(8,128)(2,1)S(1)}, u32[]{:S(2)}, u32[]{:S(2)}) collective-permute-start(bf16[48,1024]{1,0:T(8,128)(2,1)S(1)} %get-tuple-element.43), channel_id=1, source_target_pairs={{0,24},{8,16},{16,8},{24,0},{1,25},{9,17},{17,9},{25,1},{2,26},{10... | collective-permute-start | bytes 294920 | tf_op jit(solution)/shard_map/ppermute | solution.py:248
  35.6 0.2 collective-permute-start.9
  35.8 1.5 %collective-permute-start.13 = (bf16[32,1024]{1,0:T(8,128)(2,1)S(1)}, bf16[32,1024]{1,0:T(8,128)(2,1)S(1)}, u32[]{:S(2)}, u32[]{:S(2)}) collective-permute-start(bf16[32,1024]{1,0:T(8,128)(2,1)S(1)} %get-tuple-element.48), channel_id=1, source_target_pairs={{0,2},{1,3},{2,0},{3,1},{4,6},{5,7},{6,4},{7,5},{8,10},{9,11},{10,... | collective-permute-start | bytes 196616 | tf_op jit(solution)/shard_map/ppermute | solution.py:305
  37.2 0.0 collective-permute-done.12.refs_5_
  37.2 2.2 %collective-permute-start.14 = (bf16[32,1024]{1,0:T(8,128)(2,1)S(1)}, bf16[32,1024]{1,0:T(8,128)(2,1)S(1)}, u32[]{:S(2)}, u32[]{:S(2)}) collective-permute-start(bf16[32,1024]{1,0:T(8,128)(2,1)S(1)} %get-tuple-element.49), channel_id=1, source_target_pairs={{0,3},{1,2},{2,1},{3,0},{4,7},{5,6},{6,5},{7,4},{8,11},{9,10},{10,... | collective-permute-start | bytes 196616 | tf_op jit(solution)/shard_map/ppermute | solution.py:305
  39.5 0.1 shard_map.87
  39.6 0.4 collective-permute-done.13.refs_6_
  40.1 2.4 %collective-permute-done.14.refs_7_ = bf16[32,1024]{1,0:T(8,128)(2,1)S(1)} collective-permute-done((bf16[32,1024]{1,0:T(8,128)(2,1)S(1)}, bf16[32,1024]{1,0:T(8,128)(2,1)S(1)}, u32[]{:S(2)}, u32[]{:S(2)}) %collective-permute-start.14) | collective-permute-done | bytes 65568 | tf_op jit(solution)/shard_map/ppermute | solution.py:305
  42.4 0.0 collective-permute-done.10.refs_3_
  42.4 1.9 %collective-permute-done.9.refs_2_ = bf16[48,1024]{1,0:T(8,128)(2,1)S(1)} collective-permute-done((bf16[48,1024]{1,0:T(8,128)(2,1)S(1)}, bf16[48,1024]{1,0:T(8,128)(2,1)S(1)}, u32[]{:S(2)}, u32[]{:S(2)}) %collective-permute-start.9) | collective-permute-done | bytes 98336 | tf_op jit(solution)/shard_map/ppermute | solution.py:248
  44.3 0.0 collective-permute-done.8.refs_1_
  44.3 1.3 %shard_map.90 = (bf16[128,2048]{1,0:T(8,128)(2,1)}, f32[8,128]{1,0:T(8,128)}, bf16[64,384]{1,0:T(8,128)(2,1)}, f32[48,2048]{1,0:T(8,128)}) custom-call(f32[64,384]{1,0:T(8,128)S(1)} %get-tuple-element.36.keep_ref, bf16[192,128]{1,0:T(8,128)(2,1)S(1)} %get-tuple-element.37.table_ref, f32[8,128]{1,0:T(8,128)S(1)} %get-tuple-element.38.index_ref, ...), custom_call_target="tpu_custom_call" | custom-call | flops 134217728 | bytes 1941504 | tf_op jit(solution)/shard_map/pallas_call | solution.py:32
  (1 shorter events, 0.0 us)
Async XLA Ops:
  3.1 17.0 %all-to-all-start = ((bf16[8,16,1024]{2,1,0:T(8,128)(2,1)}), bf16[8,16,1024]{2,1,0:T(8,128)(2,1)S(1)}, u32[]{:S(2)}, u32[]{:S(2)}) async-start(bf16[8,16,1024]{2,1,0:T(8,128)(2,1)} %bitcast.4), calls=%async_computation | async-start | bytes 524288 | tf_op jit(solution)/shard_map/all_to_all | solution.py:255
  9.3 10.8 %collective-permute-start = (bf16[80,1024]{1,0:T(8,128)(2,1)S(1)}, bf16[80,1024]{1,0:T(8,128)(2,1)S(1)}, u32[]{:S(2)}, u32[]{:S(2)}) collective-permute-start(bf16[80,1024]{1,0:T(8,128)(2,1)S(1)} %get-tuple-element.30), channel_id=1, source_target_pairs={{0,8},{8,0},{16,24},{24,16},{1,9},{9,1},{17,25},{25,17},{2,10},{10... | collective-permute-start | bytes 491528 | tf_op jit(solution)/shard_map/ppermute | solution.py:248
  11.3 9.3 %collective-permute-start.1 = (bf16[48,1024]{1,0:T(8,128)(2,1)S(1)}, bf16[48,1024]{1,0:T(8,128)(2,1)S(1)}, u32[]{:S(2)}, u32[]{:S(2)}) collective-permute-start(bf16[48,1024]{1,0:T(8,128)(2,1)S(1)} %get-tuple-element.31), channel_id=1, source_target_pairs={{0,16},{8,24},{16,0},{24,8},{1,17},{9,25},{17,1},{25,9},{2,18},{10... | collective-permute-start | bytes 294920 | tf_op jit(solution)/shard_map/ppermute | solution.py:248
  13.9 10.3 %collective-permute-start.2 = (bf16[48,1024]{1,0:T(8,128)(2,1)S(1)}, bf16[48,1024]{1,0:T(8,128)(2,1)S(1)}, u32[]{:S(2)}, u32[]{:S(2)}) collective-permute-start(bf16[48,1024]{1,0:T(8,128)(2,1)S(1)} %get-tuple-element.32), channel_id=1, source_target_pairs={{0,24},{8,16},{16,8},{24,0},{1,25},{9,17},{17,9},{25,1},{2,26},{10... | collective-permute-start | bytes 294920 | tf_op jit(solution)/shard_map/ppermute | solution.py:248
  13.9 10.3 %collective-permute-start.3 = (bf16[80,1024]{1,0:T(8,128)(2,1)S(1)}, bf16[80,1024]{1,0:T(8,128)(2,1)S(1)}, u32[]{:S(2)}, u32[]{:S(2)}) collective-permute-start(bf16[80,1024]{1,0:T(8,128)(2,1)S(1)} %get-tuple-element.29.refs_0_), channel_id=1, source_target_pairs={{0,4},{4,0},{1,5},{5,1},{2,6},{6,2},{3,7},{7,3},{8,12},{12,8},{9,1... | collective-permute-start | bytes 491528 | tf_op jit(solution)/shard_map/ppermute | solution.py:251
  20.1 5.4 %collective-permute-start.4 = (bf16[80,1024]{1,0:T(8,128)(2,1)S(1)}, bf16[80,1024]{1,0:T(8,128)(2,1)S(1)}, u32[]{:S(2)}, u32[]{:S(2)}) collective-permute-start(bf16[80,1024]{1,0:T(8,128)(2,1)S(1)} %collective-permute-done.refs_1_), channel_id=1, source_target_pairs={{0,4},{4,0},{1,5},{5,1},{2,6},{6,2},{3,7},{7,3},{8,12},{12,8},{9,1... | collective-permute-start | bytes 491528 | tf_op jit(solution)/shard_map/ppermute | solution.py:251
  20.1 6.3 %collective-permute-start.7 = (bf16[128,1024]{1,0:T(8,128)(2,1)S(1)}, bf16[128,1024]{1,0:T(8,128)(2,1)S(1)}, u32[]{:S(2)}, u32[]{:S(2)}) collective-permute-start(bf16[128,1024]{1,0:T(8,128)(2,1)S(1)} %bitcast.9), channel_id=1, source_target_pairs={{0,4},{4,0},{1,5},{5,1},{2,6},{6,2},{3,7},{7,3},{8,12},{12,8},{9,1... | collective-permute-start | bytes 786440 | tf_op jit(solution)/shard_map/ppermute | solution.py:251
  20.6 3.6 %collective-permute-start.5 = (bf16[48,1024]{1,0:T(8,128)(2,1)S(1)}, bf16[48,1024]{1,0:T(8,128)(2,1)S(1)}, u32[]{:S(2)}, u32[]{:S(2)}) collective-permute-start(bf16[48,1024]{1,0:T(8,128)(2,1)S(1)} %collective-permute-done.1.refs_2_), channel_id=1, source_target_pairs={{0,4},{4,0},{1,5},{5,1},{2,6},{6,2},{3,7},{7,3},{8,12},{12,8},{9,1... | collective-permute-start | bytes 294920 | tf_op jit(solution)/shard_map/ppermute | solution.py:251
  24.2 1.3 %collective-permute-start.6 = (bf16[48,1024]{1,0:T(8,128)(2,1)S(1)}, bf16[48,1024]{1,0:T(8,128)(2,1)S(1)}, u32[]{:S(2)}, u32[]{:S(2)}) collective-permute-start(bf16[48,1024]{1,0:T(8,128)(2,1)S(1)} %collective-permute-done.2.refs_3_), channel_id=1, source_target_pairs={{0,4},{4,0},{1,5},{5,1},{2,6},{6,2},{3,7},{7,3},{8,12},{12,8},{9,1... | collective-permute-start | bytes 294920 | tf_op jit(solution)/shard_map/ppermute | solution.py:251
  26.3 6.4 %collective-permute-start.11 = (bf16[64,1024]{1,0:T(8,128)(2,1)S(1)}, bf16[64,1024]{1,0:T(8,128)(2,1)S(1)}, u32[]{:S(2)}, u32[]{:S(2)}) collective-permute-start(bf16[64,1024]{1,0:T(8,128)(2,1)S(1)} %get-tuple-element.45), channel_id=1, source_target_pairs={{0,8},{8,0},{1,9},{9,1},{2,10},{10,2},{3,11},{11,3},{4,12},{12,4},... | collective-permute-start | bytes 393224 | tf_op jit(solution)/shard_map/ppermute | solution.py:291
  26.9 17.4 %collective-permute-start.8 = (bf16[80,1024]{1,0:T(8,128)(2,1)S(1)}, bf16[80,1024]{1,0:T(8,128)(2,1)S(1)}, u32[]{:S(2)}, u32[]{:S(2)}) collective-permute-start(bf16[80,1024]{1,0:T(8,128)(2,1)S(1)} %get-tuple-element.41), channel_id=1, source_target_pairs={{0,8},{8,0},{16,24},{24,16},{1,9},{9,1},{17,25},{25,17},{2,10},{10... | collective-permute-start | bytes 491528 | tf_op jit(solution)/shard_map/ppermute | solution.py:248
  32.8 4.5 %collective-permute-start.12 = (bf16[32,1024]{1,0:T(8,128)(2,1)S(1)}, bf16[32,1024]{1,0:T(8,128)(2,1)S(1)}, u32[]{:S(2)}, u32[]{:S(2)}) collective-permute-start(bf16[32,1024]{1,0:T(8,128)(2,1)S(1)} %get-tuple-element.47), channel_id=1, source_target_pairs={{0,1},{1,0},{2,3},{3,2},{4,5},{5,4},{6,7},{7,6},{8,9},{9,8},{10,11... | collective-permute-start | bytes 196616 | tf_op jit(solution)/shard_map/ppermute | solution.py:305
  34.3 8.1 %collective-permute-start.10 = (bf16[48,1024]{1,0:T(8,128)(2,1)S(1)}, bf16[48,1024]{1,0:T(8,128)(2,1)S(1)}, u32[]{:S(2)}, u32[]{:S(2)}) collective-permute-start(bf16[48,1024]{1,0:T(8,128)(2,1)S(1)} %get-tuple-element.43), channel_id=1, source_target_pairs={{0,24},{8,16},{16,8},{24,0},{1,25},{9,17},{17,9},{25,1},{2,26},{10... | collective-permute-start | bytes 294920 | tf_op jit(solution)/shard_map/ppermute | solution.py:248
  35.6 8.7 %collective-permute-start.9 = (bf16[48,1024]{1,0:T(8,128)(2,1)S(1)}, bf16[48,1024]{1,0:T(8,128)(2,1)S(1)}, u32[]{:S(2)}, u32[]{:S(2)}) collective-permute-start(bf16[48,1024]{1,0:T(8,128)(2,1)S(1)} %get-tuple-element.42), channel_id=1, source_target_pairs={{0,16},{8,24},{16,0},{24,8},{1,17},{9,25},{17,1},{25,9},{2,18},{10... | collective-permute-start | bytes 294920 | tf_op jit(solution)/shard_map/ppermute | solution.py:248
  35.8 4.3 %collective-permute-start.13 = (bf16[32,1024]{1,0:T(8,128)(2,1)S(1)}, bf16[32,1024]{1,0:T(8,128)(2,1)S(1)}, u32[]{:S(2)}, u32[]{:S(2)}) collective-permute-start(bf16[32,1024]{1,0:T(8,128)(2,1)S(1)} %get-tuple-element.48), channel_id=1, source_target_pairs={{0,2},{1,3},{2,0},{3,1},{4,6},{5,7},{6,4},{7,5},{8,10},{9,11},{10,... | collective-permute-start | bytes 196616 | tf_op jit(solution)/shard_map/ppermute | solution.py:305
  37.2 5.2 %collective-permute-start.14 = (bf16[32,1024]{1,0:T(8,128)(2,1)S(1)}, bf16[32,1024]{1,0:T(8,128)(2,1)S(1)}, u32[]{:S(2)}, u32[]{:S(2)}) collective-permute-start(bf16[32,1024]{1,0:T(8,128)(2,1)S(1)} %get-tuple-element.49), channel_id=1, source_target_pairs={{0,3},{1,2},{2,1},{3,0},{4,7},{5,6},{6,5},{7,4},{8,11},{9,10},{10,... | collective-permute-start | bytes 196616 | tf_op jit(solution)/shard_map/ppermute | solution.py:305

commit v5 on v3

--- a/solution.py
+++ b/solution.py
@@ -165,9 +165,9 @@
 def expert_body(moves, groups, width, *refs):
     count = len(moves)
     blocks = refs[: 2 * count]
-    grad_ref, own_ref, other_ref, keep_ref, give_ref, hid_ref, stage_ref = refs[2 * count :]
+    own_ref, other_ref, full_ref, hid_ref, stage_ref = refs[2 * count :]
     q, h, c = lax.axis_index("q"), lax.axis_index("h"), lax.axis_index("c")
-    slots = keep_ref.shape[0]
+    slots = own_ref.shape[0]
     rows = blocks[0].shape[0] - slots // 2
     for i, (dq, dh) in enumerate(moves):
         source = (lax.rem(q + (groups - dq), groups) * 2 + lax.rem(h + dh, 2)) * 2
@@ -179,6 +179,13 @@
     out = dot(hid_ref[...], full, NN).astype(BF16)
     own_ref[...] = out[0:slots]
     other_ref[...] = out[slots:]
+    full_ref[...] = full
+
+
+def hidden_grad_body(grad_ref, full_ref, keep_ref, give_ref):
+    h = lax.axis_index("h")
+    slots = keep_ref.shape[0]
+    full = full_ref[...]
     keep_ref[...] = dot(grad_ref[aligned(h, slots, 16), :], full, NT)
     give_ref[...] = dot(grad_ref[aligned(1 - h, slots, 16), :], full, NT).astype(BF16)
 
@@ -271,16 +278,20 @@
     grads = exchange(sent)
     partner_grads = swap_core(grads)
 
-    own_out, other_out, keep, give = call(
+    own_out, other_out, full = call(
         functools.partial(expert_body, moves, groups, width),
-        (part, part, sds((slots, width), F32), sds((slots, width), BF16)),
+        (part, part, sds((width, half), BF16)),
         [
             pltpu.VMEM((2 * slots, width), BF16),
             pltpu.VMEM((width, half), BF16 if rows % 16 == 0 else F32),
         ],
         flops=8 * slots * width * half,
-    )(*blocks, grads)
+    )(*blocks)
     other_half = lax.ppermute(other_out, "h", swap)
+
+    keep, give = call(
+        hidden_grad_body, (sds((slots, width), F32), sds((slots, width), BF16)), flops=4 * slots * width * half
+    )(grads, full)
 
     weight_terms = call(
         functools.partial(weight_grad_body, moves, groups, width),

time: 45.6 us -> 44.2 us (0.969)
  waiting for transfers between devices: 18.5 us -> 17.1 us
    ppermute x3, waiting for transfers between devices: 3.69 us -> 2.86 us  [local(): arrived.append(lax.ppermute(parcels[step], 'ep', pairs))]
    ppermute x1, waiting for transfers between devices: 3.79 us -> 3.18 us  [local(): other_half = lax.ppermute(other_out, 'h', swap)]
    pallas_call x8 -> x9, Pallas kernels: 5.94 us -> 6.13 us  [run(): pl.pallas_call(body, out_shape=outs, in_specs=[inputs] * len(args), out_s...]
  transfers between devices with their start and end apart: 16 -> 16, of which waited for: 6 -> 7; matrix products, arithmetic and copies ran while one was open for 0% -> 0% of each run, Pallas kernels for 6% -> 7%
where the time goes in v5:
time: 44.2 us; the launch traced here: 43.9 us
  starting transfers between devices  20 us (45%)
  waiting for transfers between devices  17.1 us (39%)
  Pallas kernels  6.13 us (14%)
  between operations  0.71 us (2%)
    ppermute x6, waiting for transfers between devices, move(): return lax.ppermute(x, ('q', 'h'), pairs)  9.71 us
    ppermute x6, starting transfers between devices, move(): return lax.ppermute(x, ('q', 'h'), pairs)  8.7 us
    all_to_all x1, starting transfers between devices, exchange(): lax.all_to_all(parts, ('h', 'ep'), split_axis=0, concat_axis=0, tiled=True)  6.21 us
    pallas_call x9, Pallas kernels, run(): pl.pallas_call(body, out_shape=outs, in_specs=[inputs] * len(args), out_s...  6.13 us
    ppermute x3, starting transfers between devices, local(): arrived.append(lax.ppermute(parcels[step], 'ep', pairs))  4.47 us
    ppermute x1, waiting for transfers between devices, local(): other_half = lax.ppermute(other_out, 'h', swap)  3.18 us
    ppermute x3, waiting for transfers between devices, local(): arrived.append(lax.ppermute(parcels[step], 'ep', pairs))  2.86 us
    ppermute x5, waiting for transfers between devices, swap_core(): return lax.ppermute(x, 'c', swap)  1.3 us
  transfers between devices with their start and end apart: 16, of which 7 were waited for; matrix products, arithmetic and copies ran while one was open for 0% of the time, Pallas kernels for 7%

profile of v5, /device:TPU:0, one launch (start us, length us, event | category | flops | bytes accessed | tf_op | source)
XLA Modules:
  0.0 43.9 jit_solution(16397094472842022719)
XLA Ops:
  0.6 1.4 %shard_map.84 = (bf16[48,1024]{1,0:T(8,128)(2,1)S(1)}, bf16[48,1024]{1,0:T(8,128)(2,1)S(1)}, bf16[80,1024]{1,0:T(8,128)(2,1)S(1)}, bf16[80,1024]{1,0:T(8,128)(2,...) custom-call(bf16[48,2048]{1,0:T(8,128)(2,1)} %bitcast.12, s32[8,128]{1,0:T(8,128)} %bitcast.14, ...), custom_call_target="tpu_custom_call" | custom-call | bytes 2113536 | tf_op jit(solution)/shard_map/pallas_call | solution.py:31
  2.0 1.1 %shard_map.89 = bf16[128,1024]{1,0:T(8,128)(2,1)} custom-call(s32[8,128]{1,0:T(8,128)S(1)} %get-tuple-element.30.ids_ref, f32[8,128]{1,0:T(8,128)S(1)} %get-tuple-element.31.weight_ref, bf16[128,2048]{1,0:T(8,128)(2,1)S(1)} %get-tuple-element.34.cot_ref), custom_call_target="tpu_custom_call" | custom-call | flops 33554432 | bytes 524288 | tf_op jit(solution)/shard_map/pallas_call | solution.py:31
  3.1 6.2 %all-to-all-start = ((bf16[8,16,1024]{2,1,0:T(8,128)(2,1)}), bf16[8,16,1024]{2,1,0:T(8,128)(2,1)S(1)}, u32[]{:S(2)}, u32[]{:S(2)}) async-start(bf16[8,16,1024]{2,1,0:T(8,128)(2,1)} %bitcast.5), calls=%async_computation | async-start | bytes 524288 | tf_op jit(solution)/shard_map/all_to_all | solution.py:254
  9.3 2.0 %collective-permute-start = (bf16[80,1024]{1,0:T(8,128)(2,1)S(1)}, bf16[80,1024]{1,0:T(8,128)(2,1)S(1)}, u32[]{:S(2)}, u32[]{:S(2)}) collective-permute-start(bf16[80,1024]{1,0:T(8,128)(2,1)S(1)} %get-tuple-element.36), channel_id=1, source_target_pairs={{0,8},{8,0},{16,24},{24,16},{1,9},{9,1},{17,25},{25,17},{2,10},{10... | collective-permute-start | bytes 491528 | tf_op jit(solution)/shard_map/ppermute | solution.py:247
  11.3 2.6 %collective-permute-start.1 = (bf16[48,1024]{1,0:T(8,128)(2,1)S(1)}, bf16[48,1024]{1,0:T(8,128)(2,1)S(1)}, u32[]{:S(2)}, u32[]{:S(2)}) collective-permute-start(bf16[48,1024]{1,0:T(8,128)(2,1)S(1)} %get-tuple-element.37), channel_id=1, source_target_pairs={{0,16},{8,24},{16,0},{24,8},{1,17},{9,25},{17,1},{25,9},{2,18},{10... | collective-permute-start | bytes 294920 | tf_op jit(solution)/shard_map/ppermute | solution.py:247
  13.9 0.0 collective-permute-start.2
  13.9 0.0 collective-permute-start.3
  13.9 6.2 %collective-permute-done.refs_1_ = bf16[80,1024]{1,0:T(8,128)(2,1)S(1)} collective-permute-done((bf16[80,1024]{1,0:T(8,128)(2,1)S(1)}, bf16[80,1024]{1,0:T(8,128)(2,1)S(1)}, u32[]{:S(2)}, u32[]{:S(2)}) %collective-permute-start) | collective-permute-done | bytes 163872 | tf_op jit(solution)/shard_map/ppermute | solution.py:247
  20.1 0.0 collective-permute-start.4
  20.1 0.0 all-to-all-done
  20.1 0.5 %collective-permute-start.11 = (bf16[128,1024]{1,0:T(8,128)(2,1)S(1)}, bf16[128,1024]{1,0:T(8,128)(2,1)S(1)}, u32[]{:S(2)}, u32[]{:S(2)}) collective-permute-start(bf16[128,1024]{1,0:T(8,128)(2,1)S(1)} %bitcast.9), channel_id=1, source_target_pairs={{0,4},{4,0},{1,5},{5,1},{2,6},{6,2},{3,7},{7,3},{8,12},{12,8},{9,1... | collective-permute-start | bytes 786440 | tf_op jit(solution)/shard_map/ppermute | solution.py:250
  20.6 0.0 collective-permute-done.1.refs_2_
  20.6 0.1 collective-permute-start.5
  20.6 3.5 %collective-permute-done.2.refs_3_ = bf16[48,1024]{1,0:T(8,128)(2,1)S(1)} collective-permute-done((bf16[48,1024]{1,0:T(8,128)(2,1)S(1)}, bf16[48,1024]{1,0:T(8,128)(2,1)S(1)}, u32[]{:S(2)}, u32[]{:S(2)}) %collective-permute-start.2) | collective-permute-done | bytes 98336 | tf_op jit(solution)/shard_map/ppermute | solution.py:247
  24.2 0.0 collective-permute-start.6
  24.2 0.0 collective-permute-done.3.refs_4_.refs_2_
  24.2 0.0 collective-permute-done.5.refs_6_
  24.2 1.3 %collective-permute-done.6.refs_7_ = bf16[48,1024]{1,0:T(8,128)(2,1)S(1)} collective-permute-done((bf16[48,1024]{1,0:T(8,128)(2,1)S(1)}, bf16[48,1024]{1,0:T(8,128)(2,1)S(1)}, u32[]{:S(2)}, u32[]{:S(2)}) %collective-permute-start.6) | collective-permute-done | bytes 98336 | tf_op jit(solution)/shard_map/ppermute | solution.py:250
  25.5 0.0 collective-permute-done.4.refs_5_.refs_3_
  25.5 0.4 shard_map.86
  25.9 0.1 collective-permute-start.7
  26.0 0.6 %shard_map.90 = (f32[64,384]{1,0:T(8,128)S(1)}, bf16[64,384]{1,0:T(8,128)(2,1)S(1)}) custom-call(bf16[128,1024]{1,0:T(8,128)(2,1)S(1)} %bitcast.10, bf16[384,1024]{1,0:T(8,128)(2,1)S(1)} %get-tuple-element.47.full_ref), custom_call_target="tpu_custom_call" | custom-call | flops 100663296 | bytes 294912 | tf_op jit(solution)/shard_map/pallas_call | solution.py:31
  26.6 0.0 collective-permute-done.11.refs_5_
  26.6 0.5 %shard_map.91 = (f32[48,1024]{1,0:T(8,128)S(1)}, bf16[80,1024]{1,0:T(8,128)(2,1)S(1)}, bf16[48,1024]{1,0:T(8,128)(2,1)S(1)}, bf16[48,1024]{1,0:T(8,128)(2,1)S(1)}) custom-call(bf16[80,1024]{1,0:T(8,128)(2,1)S(1)} %get-tuple-element.35.refs_0_, bf16[80,1024]{1,0:T(8,128)(2,1)S(1)} %collective-permute-done.refs_1_, ...), custom_call_target="tpu_custom_call" | custom-call | flops 201326592 | bytes 1114112 | tf_op jit(solution)/shard_map/pallas_call | solution.py:31
  27.1 2.1 %collective-permute-start.12 = (bf16[80,1024]{1,0:T(8,128)(2,1)S(1)}, bf16[80,1024]{1,0:T(8,128)(2,1)S(1)}, u32[]{:S(2)}, u32[]{:S(2)}) collective-permute-start(bf16[80,1024]{1,0:T(8,128)(2,1)S(1)} %get-tuple-element.51), channel_id=1, source_target_pairs={{0,8},{8,0},{16,24},{24,16},{1,9},{9,1},{17,25},{25,17},{2,10},{10... | collective-permute-start | bytes 491528 | tf_op jit(solution)/shard_map/ppermute | solution.py:247
  29.2 3.2 %collective-permute-done.7.other_ref = bf16[64,1024]{1,0:T(8,128)(2,1)S(1)} collective-permute-done((bf16[64,1024]{1,0:T(8,128)(2,1)S(1)}, bf16[64,1024]{1,0:T(8,128)(2,1)S(1)}, u32[]{:S(2)}, u32[]{:S(2)}) %collective-permute-start.7) | collective-permute-done | bytes 131104 | tf_op jit(solution)/shard_map/ppermute | solution.py:290
  32.4 2.4 %collective-permute-start.10 = (bf16[32,1024]{1,0:T(8,128)(2,1)S(1)}, bf16[32,1024]{1,0:T(8,128)(2,1)S(1)}, u32[]{:S(2)}, u32[]{:S(2)}) collective-permute-start(bf16[32,1024]{1,0:T(8,128)(2,1)S(1)} %get-tuple-element.44), channel_id=1, source_target_pairs={{0,3},{1,2},{2,1},{3,0},{4,7},{5,6},{6,5},{7,4},{8,11},{9,10},{10,... | collective-permute-start | bytes 196616 | tf_op jit(solution)/shard_map/ppermute | solution.py:308
  34.8 0.0 collective-permute-start.13
  34.8 2.0 %collective-permute-start.14 = (bf16[48,1024]{1,0:T(8,128)(2,1)S(1)}, bf16[48,1024]{1,0:T(8,128)(2,1)S(1)}, u32[]{:S(2)}, u32[]{:S(2)}) collective-permute-start(bf16[48,1024]{1,0:T(8,128)(2,1)S(1)} %get-tuple-element.53), channel_id=1, source_target_pairs={{0,24},{8,16},{16,8},{24,0},{1,25},{9,17},{17,9},{25,1},{2,26},{10... | collective-permute-start | bytes 294920 | tf_op jit(solution)/shard_map/ppermute | solution.py:247
  36.8 0.6 %collective-permute-start.8 = (bf16[32,1024]{1,0:T(8,128)(2,1)S(1)}, bf16[32,1024]{1,0:T(8,128)(2,1)S(1)}, u32[]{:S(2)}, u32[]{:S(2)}) collective-permute-start(bf16[32,1024]{1,0:T(8,128)(2,1)S(1)} %get-tuple-element.42), channel_id=1, source_target_pairs={{0,1},{1,0},{2,3},{3,2},{4,5},{5,4},{6,7},{7,6},{8,9},{9,8},{10,11... | collective-permute-start | bytes 196616 | tf_op jit(solution)/shard_map/ppermute | solution.py:308
  37.4 0.2 collective-permute-done.10.refs_3_
  37.6 1.5 %collective-permute-start.9 = (bf16[32,1024]{1,0:T(8,128)(2,1)S(1)}, bf16[32,1024]{1,0:T(8,128)(2,1)S(1)}, u32[]{:S(2)}, u32[]{:S(2)}) collective-permute-start(bf16[32,1024]{1,0:T(8,128)(2,1)S(1)} %get-tuple-element.43), channel_id=1, source_target_pairs={{0,2},{1,3},{2,0},{3,1},{4,6},{5,7},{6,4},{7,5},{8,10},{9,11},{10,... | collective-permute-start | bytes 196616 | tf_op jit(solution)/shard_map/ppermute | solution.py:308
  39.1 0.1 shard_map.85
  39.2 1.9 %collective-permute-done.8.refs_1_ = bf16[32,1024]{1,0:T(8,128)(2,1)S(1)} collective-permute-done((bf16[32,1024]{1,0:T(8,128)(2,1)S(1)}, bf16[32,1024]{1,0:T(8,128)(2,1)S(1)}, u32[]{:S(2)}, u32[]{:S(2)}) %collective-permute-start.8) | collective-permute-done | bytes 65568 | tf_op jit(solution)/shard_map/ppermute | solution.py:308
  41.1 0.8 %collective-permute-done.9.refs_2_ = bf16[32,1024]{1,0:T(8,128)(2,1)S(1)} collective-permute-done((bf16[32,1024]{1,0:T(8,128)(2,1)S(1)}, bf16[32,1024]{1,0:T(8,128)(2,1)S(1)}, u32[]{:S(2)}, u32[]{:S(2)}) %collective-permute-start.9) | collective-permute-done | bytes 65568 | tf_op jit(solution)/shard_map/ppermute | solution.py:308
  41.9 1.2 %shard_map.88 = (bf16[128,2048]{1,0:T(8,128)(2,1)}, f32[8,128]{1,0:T(8,128)}) custom-call(bf16[192,128]{1,0:T(8,128)(2,1)S(1)} %get-tuple-element.32.table_ref, f32[8,128]{1,0:T(8,128)S(1)} %get-tuple-element.33.index_ref, bf16[128,2048]{1,0:T(8,128)(2,1)S(1)} %get-tuple-element.34.cot_ref, bf16[32,1024]{1,0:T(8,128)(2,1)S(1)} %get-tuple-element.41.refs_0_, ...), custom_call_target="tpu_custom_call" | custom-call | flops 134217728 | bytes 1056768 | tf_op jit(solution)/shard_map/pallas_call | solution.py:31
  43.1 0.0 collective-permute-done.13.refs_2_
  43.1 0.0 collective-permute-done.14.refs_3_
  43.1 0.0 collective-permute-done.12.refs_1_
  43.1 0.8 %shard_map.92 = (bf16[64,384]{1,0:T(8,128)(2,1)}, f32[48,2048]{1,0:T(8,128)}) custom-call(f32[64,384]{1,0:T(8,128)S(1)} %get-tuple-element.48.keep_ref, f32[48,1024]{1,0:T(8,128)S(1)} %get-tuple-element.50.refs_0_, bf16[80,1024]{1,0:T(8,128)(2,1)S(1)} %collective-permute-done.12.refs_1_, bf16[48,1024]{1,0:T(8,128)(2,1)S(1)} %collective-permute-done.13.refs_2_, ...), custom_call_target="tpu_custom_call" | custom-call | flops 98304 | bytes 884736 | tf_op jit(solution)/shard_map/pallas_call | solution.py:31
  (1 shorter events, 0.0 us)
Async XLA Ops:
  3.1 17.0 %all-to-all-start = ((bf16[8,16,1024]{2,1,0:T(8,128)(2,1)}), bf16[8,16,1024]{2,1,0:T(8,128)(2,1)S(1)}, u32[]{:S(2)}, u32[]{:S(2)}) async-start(bf16[8,16,1024]{2,1,0:T(8,128)(2,1)} %bitcast.5), calls=%async_computation | async-start | bytes 524288 | tf_op jit(solution)/shard_map/all_to_all | solution.py:254
  9.3 10.8 %collective-permute-start = (bf16[80,1024]{1,0:T(8,128)(2,1)S(1)}, bf16[80,1024]{1,0:T(8,128)(2,1)S(1)}, u32[]{:S(2)}, u32[]{:S(2)}) collective-permute-start(bf16[80,1024]{1,0:T(8,128)(2,1)S(1)} %get-tuple-element.36), channel_id=1, source_target_pairs={{0,8},{8,0},{16,24},{24,16},{1,9},{9,1},{17,25},{25,17},{2,10},{10... | collective-permute-start | bytes 491528 | tf_op jit(solution)/shard_map/ppermute | solution.py:247
  11.3 9.3 %collective-permute-start.1 = (bf16[48,1024]{1,0:T(8,128)(2,1)S(1)}, bf16[48,1024]{1,0:T(8,128)(2,1)S(1)}, u32[]{:S(2)}, u32[]{:S(2)}) collective-permute-start(bf16[48,1024]{1,0:T(8,128)(2,1)S(1)} %get-tuple-element.37), channel_id=1, source_target_pairs={{0,16},{8,24},{16,0},{24,8},{1,17},{9,25},{17,1},{25,9},{2,18},{10... | collective-permute-start | bytes 294920 | tf_op jit(solution)/shard_map/ppermute | solution.py:247
  13.9 10.3 %collective-permute-start.2 = (bf16[48,1024]{1,0:T(8,128)(2,1)S(1)}, bf16[48,1024]{1,0:T(8,128)(2,1)S(1)}, u32[]{:S(2)}, u32[]{:S(2)}) collective-permute-start(bf16[48,1024]{1,0:T(8,128)(2,1)S(1)} %get-tuple-element.38), channel_id=1, source_target_pairs={{0,24},{8,16},{16,8},{24,0},{1,25},{9,17},{17,9},{25,1},{2,26},{10... | collective-permute-start | bytes 294920 | tf_op jit(solution)/shard_map/ppermute | solution.py:247
  13.9 10.3 %collective-permute-start.3 = (bf16[80,1024]{1,0:T(8,128)(2,1)S(1)}, bf16[80,1024]{1,0:T(8,128)(2,1)S(1)}, u32[]{:S(2)}, u32[]{:S(2)}) collective-permute-start(bf16[80,1024]{1,0:T(8,128)(2,1)S(1)} %get-tuple-element.35.refs_0_), channel_id=1, source_target_pairs={{0,4},{4,0},{1,5},{5,1},{2,6},{6,2},{3,7},{7,3},{8,12},{12,8},{9,1... | collective-permute-start | bytes 491528 | tf_op jit(solution)/shard_map/ppermute | solution.py:250
  20.1 5.4 %collective-permute-start.4 = (bf16[80,1024]{1,0:T(8,128)(2,1)S(1)}, bf16[80,1024]{1,0:T(8,128)(2,1)S(1)}, u32[]{:S(2)}, u32[]{:S(2)}) collective-permute-start(bf16[80,1024]{1,0:T(8,128)(2,1)S(1)} %collective-permute-done.refs_1_), channel_id=1, source_target_pairs={{0,4},{4,0},{1,5},{5,1},{2,6},{6,2},{3,7},{7,3},{8,12},{12,8},{9,1... | collective-permute-start | bytes 491528 | tf_op jit(solution)/shard_map/ppermute | solution.py:250
  20.1 6.5 %collective-permute-start.11 = (bf16[128,1024]{1,0:T(8,128)(2,1)S(1)}, bf16[128,1024]{1,0:T(8,128)(2,1)S(1)}, u32[]{:S(2)}, u32[]{:S(2)}) collective-permute-start(bf16[128,1024]{1,0:T(8,128)(2,1)S(1)} %bitcast.9), channel_id=1, source_target_pairs={{0,4},{4,0},{1,5},{5,1},{2,6},{6,2},{3,7},{7,3},{8,12},{12,8},{9,1... | collective-permute-start | bytes 786440 | tf_op jit(solution)/shard_map/ppermute | solution.py:250
  20.6 3.6 %collective-permute-start.5 = (bf16[48,1024]{1,0:T(8,128)(2,1)S(1)}, bf16[48,1024]{1,0:T(8,128)(2,1)S(1)}, u32[]{:S(2)}, u32[]{:S(2)}) collective-permute-start(bf16[48,1024]{1,0:T(8,128)(2,1)S(1)} %collective-permute-done.1.refs_2_), channel_id=1, source_target_pairs={{0,4},{4,0},{1,5},{5,1},{2,6},{6,2},{3,7},{7,3},{8,12},{12,8},{9,1... | collective-permute-start | bytes 294920 | tf_op jit(solution)/shard_map/ppermute | solution.py:250
  24.2 1.3 %collective-permute-start.6 = (bf16[48,1024]{1,0:T(8,128)(2,1)S(1)}, bf16[48,1024]{1,0:T(8,128)(2,1)S(1)}, u32[]{:S(2)}, u32[]{:S(2)}) collective-permute-start(bf16[48,1024]{1,0:T(8,128)(2,1)S(1)} %collective-permute-done.2.refs_3_), channel_id=1, source_target_pairs={{0,4},{4,0},{1,5},{5,1},{2,6},{6,2},{3,7},{7,3},{8,12},{12,8},{9,1... | collective-permute-start | bytes 294920 | tf_op jit(solution)/shard_map/ppermute | solution.py:250
  25.9 6.4 %collective-permute-start.7 = (bf16[64,1024]{1,0:T(8,128)(2,1)S(1)}, bf16[64,1024]{1,0:T(8,128)(2,1)S(1)}, u32[]{:S(2)}, u32[]{:S(2)}) collective-permute-start(bf16[64,1024]{1,0:T(8,128)(2,1)S(1)} %get-tuple-element.40), channel_id=1, source_target_pairs={{0,8},{8,0},{1,9},{9,1},{2,10},{10,2},{3,11},{11,3},{4,12},{12,4},... | collective-permute-start | bytes 393224 | tf_op jit(solution)/shard_map/ppermute | solution.py:290
  27.1 16.0 %collective-permute-start.12 = (bf16[80,1024]{1,0:T(8,128)(2,1)S(1)}, bf16[80,1024]{1,0:T(8,128)(2,1)S(1)}, u32[]{:S(2)}, u32[]{:S(2)}) collective-permute-start(bf16[80,1024]{1,0:T(8,128)(2,1)S(1)} %get-tuple-element.51), channel_id=1, source_target_pairs={{0,8},{8,0},{16,24},{24,16},{1,9},{9,1},{17,25},{25,17},{2,10},{10... | collective-permute-start | bytes 491528 | tf_op jit(solution)/shard_map/ppermute | solution.py:247
  32.4 5.2 %collective-permute-start.10 = (bf16[32,1024]{1,0:T(8,128)(2,1)S(1)}, bf16[32,1024]{1,0:T(8,128)(2,1)S(1)}, u32[]{:S(2)}, u32[]{:S(2)}) collective-permute-start(bf16[32,1024]{1,0:T(8,128)(2,1)S(1)} %get-tuple-element.44), channel_id=1, source_target_pairs={{0,3},{1,2},{2,1},{3,0},{4,7},{5,6},{6,5},{7,4},{8,11},{9,10},{10,... | collective-permute-start | bytes 196616 | tf_op jit(solution)/shard_map/ppermute | solution.py:308
  34.8 8.3 %collective-permute-start.13 = (bf16[48,1024]{1,0:T(8,128)(2,1)S(1)}, bf16[48,1024]{1,0:T(8,128)(2,1)S(1)}, u32[]{:S(2)}, u32[]{:S(2)}) collective-permute-start(bf16[48,1024]{1,0:T(8,128)(2,1)S(1)} %get-tuple-element.52), channel_id=1, source_target_pairs={{0,16},{8,24},{16,0},{24,8},{1,17},{9,25},{17,1},{25,9},{2,18},{10... | collective-permute-start | bytes 294920 | tf_op jit(solution)/shard_map/ppermute | solution.py:247
  34.8 8.3 %collective-permute-start.14 = (bf16[48,1024]{1,0:T(8,128)(2,1)S(1)}, bf16[48,1024]{1,0:T(8,128)(2,1)S(1)}, u32[]{:S(2)}, u32[]{:S(2)}) collective-permute-start(bf16[48,1024]{1,0:T(8,128)(2,1)S(1)} %get-tuple-element.53), channel_id=1, source_target_pairs={{0,24},{8,16},{16,8},{24,0},{1,25},{9,17},{17,9},{25,1},{2,26},{10... | collective-permute-start | bytes 294920 | tf_op jit(solution)/shard_map/ppermute | solution.py:247
  36.8 4.3 %collective-permute-start.8 = (bf16[32,1024]{1,0:T(8,128)(2,1)S(1)}, bf16[32,1024]{1,0:T(8,128)(2,1)S(1)}, u32[]{:S(2)}, u32[]{:S(2)}) collective-permute-start(bf16[32,1024]{1,0:T(8,128)(2,1)S(1)} %get-tuple-element.42), channel_id=1, source_target_pairs={{0,1},{1,0},{2,3},{3,2},{4,5},{5,4},{6,7},{7,6},{8,9},{9,8},{10,11... | collective-permute-start | bytes 196616 | tf_op jit(solution)/shard_map/ppermute | solution.py:308
  37.6 4.3 %collective-permute-start.9 = (bf16[32,1024]{1,0:T(8,128)(2,1)S(1)}, bf16[32,1024]{1,0:T(8,128)(2,1)S(1)}, u32[]{:S(2)}, u32[]{:S(2)}) collective-permute-start(bf16[32,1024]{1,0:T(8,128)(2,1)S(1)} %get-tuple-element.43), channel_id=1, source_target_pairs={{0,2},{1,3},{2,0},{3,1},{4,6},{5,7},{6,4},{7,5},{8,10},{9,11},{10,... | collective-permute-start | bytes 196616 | tf_op jit(solution)/shard_map/ppermute | solution.py:308
